TPU v7x, 128 devices: a whole 4x4x4 slice. The times are simulated.
128 devices in a mesh: grp: 4 (over z), leaf: 32 (over y, x, core).
Axes of the slice: x: 4, y: 4, z: 4, core: 2. Of those that a mesh axis runs over, the one named last changes fastest.
Arguments:
- basis_slab: bfloat16 [131072, 1024], P(('grp', 'leaf')), may hold values from -6 to 6
- live_counts: int32 [128], P(('grp', 'leaf')), may hold values from 128 to 1024, as said below
- pole_order: int32 [128, 1024], P(('grp', 'leaf')), may hold values from 0 to 1023, each once within a row
- leaf_diag: bfloat16 [131072, 1024], P(('grp', 'leaf')), may hold values from -0.1875 to 0.1875
- leaf_in: bfloat16 [131072, 128], P(('grp', 'leaf')), may hold values from -0.1875 to 0.1875
- leaf_out: bfloat16 [131072, 128], P(('grp', 'leaf')), may hold values from -0.5 to 0.5
- leaf_lift: bfloat16 [128, 128, 128], P(('grp', 'leaf')), may hold values from -0.375 to 0.375
- leaf_couple: bfloat16 [128, 128, 128], P(('grp', 'leaf')), may hold values from -0.5 to 0.5
- leaf_spread: bfloat16 [128, 128, 128], P(('grp', 'leaf')), may hold values from -0.4375 to 0.4375
- inner_lift: bfloat16 [124, 128, 128], replicated, may hold values from -0.375 to 0.375
- inner_couple: bfloat16 [126, 128, 128], replicated, may hold values from -0.5 to 0.5
- inner_spread: bfloat16 [124, 128, 128], replicated, may hold values from -0.4375 to 0.4375
Outputs:
- merged: bfloat16 [131072, 1024], P(('grp', 'leaf'))
Inputs may be any that keep to these rules, and one draw needn't show every extreme that they name: `live_counts`: each count is 1024, 512, 256 or 128, and some leaf has 1024. `pole_order`: each row names every slot's pole once.
All inputs are finite; a program needn't handle non-finite values.
Results may differ from a plain program's by a relative error of at most 0.0055.
Values may be sent and summed in bfloat16 or wider, within the bound.
No kernel may reach another device: no remote copies, remote signals or barrier semaphores. Data moves between devices by JAX's collectives and lax.ppermute only.
A program may use at most 64 MiB of HBM per device.

v0:
```python
import jax
import jax.numpy as jnp
from jax import lax
from jax.sharding import PartitionSpec as P


def from_partner(block, axis, apart):
    count = lax.axis_size(axis)
    route = []
    for low in range(count):
        high = low | 1 << apart
        if high != low and high < count:
            route += [(low, high), (high, low)]
    return lax.ppermute(block, axis, route)


def from_everyone(array, axis):
    peers = lax.axis_size(axis)
    return lax.all_to_all(
        jnp.broadcast_to(array[None], (peers, *array.shape)), axis, 0, 0, tiled=True
    )


def in_order(tiles, dim):
    tiles = jnp.moveaxis(tiles, 0, dim)
    lengths = tiles.shape
    return tiles.reshape(*lengths[:dim], lengths[dim] * lengths[dim + 1], *lengths[dim + 2 :])


def gathered_copies(array, axis, dim):
    tiles = from_everyone(array, axis)
    return in_order(tiles, dim)


def transform(matrix, stacked):
    return jnp.dot(matrix.astype(jnp.float32), stacked, precision=lax.Precision.HIGHEST)


def local(
    basis_slab,
    live_counts,
    pole_order,
    leaf_diag,
    leaf_in,
    leaf_out,
    leaf_lift,
    leaf_couple,
    leaf_spread,
    inner_lift,
    inner_couple,
    inner_spread,
):
    groups = lax.axis_size("grp")
    leaves = lax.axis_size("leaf")
    devices = groups * leaves
    leaf_width = basis_slab.shape[0]
    slab_rows = basis_slab.shape[1]
    block_rows = leaf_width // devices
    levels = devices.bit_length() - 1
    leaf_bits = leaves.bit_length() - 1
    position = lax.axis_index("grp") * leaves + lax.axis_index("leaf")

    def redistribute(columns):
        arrived = lax.all_to_all(
            columns.reshape(devices, block_rows, slab_rows),
            ("grp", "leaf"),
            split_axis=0,
            concat_axis=0,
            tiled=True,
        )
        return arrived.reshape(leaf_width, slab_rows)

    def node_matrix(height, leaf_table, inner_table, offset):
        if height == 0:
            return leaf_table[0]
        own_node = jnp.right_shift(devices + position, height)
        return lax.dynamic_index_in_dim(inner_table, own_node - offset, 0, keepdims=False)

    def sibling_matrix(height, inner_table, offset):
        sibling_node = jnp.bitwise_xor(jnp.right_shift(devices + position, height), 1)
        return lax.dynamic_index_in_dim(inner_table, sibling_node - offset, 0, keepdims=False)

    leaf_rows = redistribute(basis_slab)
    slot_order = pole_order[0]
    live_count = live_counts[0]
    slots = jnp.take(leaf_rows, slot_order, axis=0)
    live_mask = jnp.arange(leaf_width, dtype=jnp.int32) < live_count
    masked = jnp.where(live_mask[:, None], slots, jnp.zeros_like(slots))
    skeleton = jnp.einsum("mk,mc->kc", leaf_in, masked, preferred_element_type=jnp.float32)
    crosses = []
    other_skeleton, other_lift_matrix, other_couple_matrix = from_partner(
        (skeleton, leaf_lift[0].astype(jnp.float32), leaf_couple[0].astype(jnp.float32)), "leaf", 0
    )
    crosses.append(transform(other_couple_matrix, other_skeleton))
    skeleton = transform(leaf_lift[0], skeleton) + transform(other_lift_matrix, other_skeleton)
    for height in range(1, leaf_bits):
        other_skeleton = from_partner(skeleton, "leaf", height)
        crosses.append(transform(sibling_matrix(height, inner_couple, 2), other_skeleton))
        skeleton = transform(node_matrix(height, leaf_lift, inner_lift, 4), skeleton) + transform(
            sibling_matrix(height, inner_lift, 4), other_skeleton
        )
    nodes_now = gathered_copies(skeleton[None].astype(jnp.bfloat16), "grp", 0).astype(jnp.float32)
    for height in range(leaf_bits, levels):
        base_node = devices >> height
        sibling = jnp.bitwise_xor(jnp.right_shift(position, height), 1)
        couple_matrix = lax.dynamic_index_in_dim(
            inner_couple, base_node + sibling - 2, 0, keepdims=False
        )
        sibling_skeleton = lax.dynamic_index_in_dim(nodes_now, sibling, 0, keepdims=False)
        crosses.append(transform(couple_matrix, sibling_skeleton))
        if height < levels - 1:
            lifts = inner_lift[base_node - 4 : 2 * base_node - 4].astype(jnp.float32)
            lifted = jnp.einsum("nij,njc->nic", lifts, nodes_now, precision=lax.Precision.HIGHEST)
            nodes_now = lifted[0::2] + lifted[1::2]
    incoming = crosses[levels - 1]
    for height in range(levels - 2, -1, -1):
        incoming = (
            transform(node_matrix(height, leaf_spread, inner_spread, 4), incoming) + crosses[height]
        )
    incoming_b = incoming.astype(jnp.bfloat16)
    tile_rows = leaf_width // 8
    tile_count = live_count // tile_rows

    def one_tile(tile_index, merged_rows):
        row_start = tile_index * tile_rows
        diag_rows = lax.dynamic_slice_in_dim(leaf_diag, row_start, tile_rows, 0)
        out_rows = lax.dynamic_slice_in_dim(leaf_out, row_start, tile_rows, 0)
        value = jnp.dot(diag_rows, masked, preferred_element_type=jnp.float32) + jnp.dot(
            out_rows, incoming_b, preferred_element_type=jnp.float32
        )
        return lax.dynamic_update_slice_in_dim(merged_rows, value, row_start, 0)

    merged_rows = lax.fori_loop(
        0, tile_count, one_tile, jnp.zeros((leaf_width, slab_rows), jnp.float32)
    )
    updated = jnp.where(live_mask[:, None], merged_rows, slots.astype(jnp.float32)).astype(
        jnp.bfloat16
    )
    inverse = (
        jnp.zeros((leaf_width,), jnp.int32)
        .at[slot_order]
        .set(jnp.arange(leaf_width, dtype=jnp.int32))
    )
    restored = jnp.take(updated, inverse, axis=0)
    return redistribute(restored)


def solution(mesh):
    placed = (
        P(("grp", "leaf"), None),
        P(("grp", "leaf")),
        P(("grp", "leaf"), None),
        P(("grp", "leaf"), None),
        P(("grp", "leaf"), None),
        P(("grp", "leaf"), None),
        P(("grp", "leaf"), None, None),
        P(("grp", "leaf"), None, None),
        P(("grp", "leaf"), None, None),
        P(),
        P(),
        P(),
    )
    return jax.shard_map(
        local, mesh=mesh, in_specs=placed, out_specs=P(("grp", "leaf"), None), check_vma=False
    )
```

profile of v0, /device:TPU:1, one launch (start us, length us, event | category | flops | bytes accessed | tf_op | source)
XLA Modules:
  0.0 220.5 jit_solution(9666176202638816031)
XLA Ops:
  0.0 11.5 %all-to-all-start = ((bf16[128,8,1024]{2,1,0:T(8,128)(2,1)}), bf16[128,8,1024]{2,1,0:T(8,128)(2,1)S(1)}, u32[]{:S(2)}, u32[]{:S(2)}) async-start(bf16[128,8,1024]{2,1,0:T(8,128)(2,1)} %bitcast.132), calls=%async_computation | async-start | bytes 4194304 | tf_op jit(solution)/shard_map/all_to_all | solution.py:64
  12.2 29.8 %all-to-all-done = bf16[128,8,1024]{2,1,0:T(8,128)(2,1)S(1)} async-done(((bf16[128,8,1024]{2,1,0:T(8,128)(2,1)}), bf16[128,8,1024]{2,1,0:T(8,128)(2,1)S(1)}, u32[]{:S(2)}, u32[]{:S(2)}) %all-to-all-start) | async-done | bytes 2097184 | tf_op jit(solution)/shard_map/all_to_all | solution.py:64
  42.0 5.3 %gather_fusion = bf16[1024,1024]{1,0:T(8,128)(2,1)} fusion(bf16[1024,1024]{1,0:T(8,128)(2,1)S(1)} %bitcast.128, s32[1024]{0:T(1024)S(1)} %fusion.87), kind=kCustom, calls=%fused_computation.clone | custom fusion | bytes 4198400 | tf_op jit(solution)/shard_map/jit(_take)/gather | solution.py:86
  47.3 2.1 broadcast_select_fusion.1
  55.8 11.6 %collective-permute-done.2 = f32[128,1024]{0,1:T(8,128)S(1)} collective-permute-done((f32[128,1024]{0,1:T(8,128)S(1)}, f32[128,1024]{0,1:T(8,128)S(1)}, u32[]{:S(2)}, u32[]{:S(2)}) %collective-permute-start.2) | collective-permute-done | bytes 524320 | tf_op jit(solution)/shard_map/ppermute | solution.py:14
  67.4 2.0 convolution_add_fusion.10
  69.7 1.5 fusion.32
  71.2 12.2 %collective-permute-done.3 = f32[128,1024]{1,0:T(8,128)S(1)} collective-permute-done((f32[128,1024]{1,0:T(8,128)}, f32[128,1024]{1,0:T(8,128)S(1)}, u32[]{:S(2)}, u32[]{:S(2)}) %collective-permute-start.3) | collective-permute-done | bytes 524320 | tf_op jit(solution)/shard_map/ppermute | solution.py:14
  83.4 2.0 convolution_add_fusion.9
  86.8 10.2 %collective-permute-done.4 = f32[128,1024]{1,0:T(8,128)} collective-permute-done((f32[128,1024]{1,0:T(8,128)}, f32[128,1024]{1,0:T(8,128)}, u32[]{:S(2)}, u32[]{:S(2)}) %collective-permute-start.4) | collective-permute-done | bytes 524320 | tf_op jit(solution)/shard_map/ppermute | solution.py:14
  100.1 10.6 %collective-permute-done.5 = f32[128,1024]{1,0:T(8,128)S(1)} collective-permute-done((f32[128,1024]{1,0:T(8,128)S(1)}, f32[128,1024]{1,0:T(8,128)S(1)}, u32[]{:S(2)}, u32[]{:S(2)}) %collective-permute-start.5) | collective-permute-done | bytes 524320 | tf_op jit(solution)/shard_map/ppermute | solution.py:14
  113.1 3.5 %all-to-all-start.1 = ((bf16[4,1,128,1024]{2,3,1,0:T(8,128)(2,1)}), bf16[4,1,128,1024]{2,3,1,0:T(8,128)(2,1)S(1)}, u32[]{:S(2)}, u32[]{:S(2)}) async-start(bf16[4,1,128,1024]{2,3,1,0:T(8,128)(2,1)} %broadcast_in_dim.42), calls=%async_computation.1 | async-start | bytes 2097152 | tf_op jit(solution)/shard_map/all_to_all | solution.py:19
  116.7 3.9 %collective-permute-start.6 = (f32[128,128]{1,0:T(8,128)S(1)}, f32[128,128]{1,0:T(8,128)S(1)}, u32[]{:S(2)}, u32[]{:S(2)}) collective-permute-start(f32[128,128]{1,0:T(8,128)S(1)} %bitcast_convert_fusion), channel_id=1, source_target_pairs={{0,1},{1,0},{2,3},{3,2},{4,5},{5,4},{6,7},{7,6},{8,9},{9,8},{10,11... | collective-permute-start | bytes 196616 | tf_op jit(solution)/shard_map/ppermute | solution.py:14
  121.1 4.6 %scatter_custom_fusion = s32[1024]{0:T(1024)S(1)} fusion(s32[1024]{0:T(1024)S(1)} %bitcast.135, s32[1024]{0:T(1024)} %iota.9, s32[]{:T(128)} %constant.129.clone.1), kind=kCustom, calls=%fused_computation.117 | custom fusion | bytes 4608 | tf_op jit(solution)/shard_map/scatter | solution.py:142
  143.9 1.6 broadcast_in_dim.40
  145.5 12.3 %while.10 = (s32[]{:T(128)}, bf16[1024,1024]{1,0:T(8,128)(2,1)}, s32[]{:T(128)}, bf16[1024,1024]{1,0:T(8,128)(2,1)}, bf16[1024,1024]{1,0:T(8,128)(2,1)S(1)}, /*i...) while((s32[]{:T(128)}, bf16[1024,1024]{1,0:T(8,128)(2,1)}, ...), condition=%wide.region_1.3_spmd, body=%wide.region_0.0_spmd.sunk | while | flops 302120960 | bytes 4228255 | solution.py:133
  146.9 1.7 fusion.131
  149.9 1.7 fusion.131
  153.0 1.7 fusion.131
  156.1 1.7 fusion.131
  157.8 2.7 %select_convert_fusion = bf16[1024,1024]{1,0:T(8,128)(2,1)S(1)} fusion(bf16[1024,1024]{1,0:T(8,128)(2,1)} %get-tuple-element.44, pred[1024]{0:T(1024)(128)(4,1)S(1)} %get-tuple-element.82, bf16[1024,1024]{1,0:T(8,128)(2,1)} %gather_fusion, pred[1024]{0:T(1024)(128)(4,1)S(1)} %get-tuple-element.83), kind=kLoop, calls=%fused_computation.10 | loop fusion | flops 3145728 | bytes 6293504 | tf_op jit(solution)/shard_map/convert_element_type | solution.py:136
  160.5 5.3 %gather_fusion.1 = bf16[1024,1024]{1,0:T(8,128)(2,1)} fusion(bf16[1024,1024]{1,0:T(8,128)(2,1)S(1)} %select_convert_fusion, s32[1024]{0:T(1024)S(1)} %fusion.88), kind=kCustom, calls=%fused_computation.1.clone | custom fusion | bytes 4198400 | tf_op jit(solution)/shard_map/jit(_take)/gather | solution.py:144
  165.9 1.9 select_bitcast_fusion
  167.7 51.4 %all_to_all.15 = bf16[128,8,1024]{2,1,0:T(8,128)(2,1)S(1)} all-to-all(bf16[128,8,1024]{2,1,0:T(8,128)(2,1)S(1)} %select_bitcast_fusion), channel_id=1, replica_groups=mesh['grp'=4,'leaf'=32] {'grp','leaf'}, dimensions={0} | all-to-all | bytes 4194304 | tf_op jit(solution)/shard_map/all_to_all | solution.py:64
  (77 shorter events, 39.0 us)
Async XLA Ops:
  0.0 49.4 %copy-start = (bf16[1024,128]{1,0:T(8,128)(2,1)S(1)}, bf16[1024,128]{1,0:T(8,128)(2,1)}, u32[]{:S(2)}) copy-start(bf16[1024,128]{1,0:T(8,128)(2,1)} %param.20) | copy-start | bytes 786436
  0.0 12.1 %copy-start.10 = (s32[1,1024]{1,0:T(1,128)S(1)}, s32[1,1024]{1,0:T(1,128)}, u32[]{:S(2)}) copy-start(s32[1,1024]{1,0:T(1,128)} %param.18) | copy-start | bytes 12292
  0.0 42.0 %all-to-all-start = ((bf16[128,8,1024]{2,1,0:T(8,128)(2,1)}), bf16[128,8,1024]{2,1,0:T(8,128)(2,1)S(1)}, u32[]{:S(2)}, u32[]{:S(2)}) async-start(bf16[128,8,1024]{2,1,0:T(8,128)(2,1)} %bitcast.132), calls=%async_computation | async-start | bytes 4194304 | tf_op jit(solution)/shard_map/all_to_all | solution.py:64
  49.4 1.8 copy-start.9
  50.2 2.7 %collective-permute-start = (f32[128,1024]{0,1:T(8,128)S(1)}, f32[128,1024]{0,1:T(8,128)S(1)}, u32[]{:S(2)}, u32[]{:S(2)}) collective-permute-start(f32[128,1024]{0,1:T(8,128)S(1)} %bitcast.130), channel_id=1, source_target_pairs={{0,1},{1,0},{2,3},{3,2},{4,5},{5,4},{6,7},{7,6},{8,9},{9,8},{10,11... | collective-permute-start | bytes 1572872 | tf_op jit(solution)/shard_map/ppermute | solution.py:14
  51.2 1.6 collective-permute-start.1
  52.8 0.8 copy-start.1
  54.2 13.2 %collective-permute-start.2 = (f32[128,1024]{0,1:T(8,128)S(1)}, f32[128,1024]{0,1:T(8,128)S(1)}, u32[]{:S(2)}, u32[]{:S(2)}) collective-permute-start(f32[128,1024]{0,1:T(8,128)S(1)} %bitcast.131), channel_id=1, source_target_pairs={{0,2},{2,0},{1,3},{3,1},{4,6},{6,4},{5,7},{7,5},{8,10},{10,8},{9,1... | collective-permute-start | bytes 1572872 | tf_op jit(solution)/shard_map/ppermute | solution.py:14
  67.4 17.9 %copy-start.5 = (f32[128,1024]{0,1:T(8,128)}, f32[128,1024]{0,1:T(8,128)S(1)}, u32[]{:S(2)}) copy-start(f32[128,1024]{0,1:T(8,128)S(1)} %collective-permute-done.2) | copy-start | bytes 1572868
  69.4 14.0 %collective-permute-start.3 = (f32[128,1024]{1,0:T(8,128)}, f32[128,1024]{1,0:T(8,128)S(1)}, u32[]{:S(2)}, u32[]{:S(2)}) collective-permute-start(f32[128,1024]{1,0:T(8,128)} %convolution_add_fusion.10), channel_id=1, source_target_pairs={{0,4},{4,0},{1,5},{5,1},{2,6},{6,2},{3,7},{7,3},{8,12},{12,8},{9,1... | collective-permute-start | bytes 1572872 | tf_op jit(solution)/shard_map/ppermute | solution.py:14
  83.4 13.7 %copy-start.7 = (f32[128,1024]{1,0:T(8,128)}, f32[128,1024]{1,0:T(8,128)S(1)}, u32[]{:S(2)}) copy-start(f32[128,1024]{1,0:T(8,128)S(1)} %collective-permute-done.3) | copy-start | bytes 1572868
  85.3 11.7 %collective-permute-start.4 = (f32[128,1024]{1,0:T(8,128)}, f32[128,1024]{1,0:T(8,128)}, u32[]{:S(2)}, u32[]{:S(2)}) collective-permute-start(f32[128,1024]{1,0:T(8,128)} %convolution_add_fusion.9), channel_id=1, source_target_pairs={{0,8},{8,0},{1,9},{9,1},{2,10},{10,2},{3,11},{11,3},{4,12},{12,4},... | collective-permute-start | bytes 1572872 | tf_op jit(solution)/shard_map/ppermute | solution.py:14
  98.5 12.1 %collective-permute-start.5 = (f32[128,1024]{1,0:T(8,128)S(1)}, f32[128,1024]{1,0:T(8,128)S(1)}, u32[]{:S(2)}, u32[]{:S(2)}) collective-permute-start(f32[128,1024]{1,0:T(8,128)S(1)} %convolution_add_fusion.8), channel_id=1, source_target_pairs={{0,16},{16,0},{1,17},{17,1},{2,18},{18,2},{3,19},{19,3},{4,20},{20... | collective-permute-start | bytes 1572872 | tf_op jit(solution)/shard_map/ppermute | solution.py:14
  110.6 2.5 %copy-start.3 = (f32[128,1024]{1,0:T(8,128)}, f32[128,1024]{1,0:T(8,128)S(1)}, u32[]{:S(2)}) copy-start(f32[128,1024]{1,0:T(8,128)S(1)} %collective-permute-done.5) | copy-start | bytes 1572868
  111.8 4.8 %copy-start.11 = (bf16[1,128,128]{2,1,0:T(8,128)(2,1)S(1)}, bf16[1,128,128]{2,1,0:T(8,128)(2,1)}, u32[]{:S(2)}) copy-start(bf16[1,128,128]{2,1,0:T(8,128)(2,1)} %param.23) | copy-start | bytes 98308
  113.1 14.6 %all-to-all-start.1 = ((bf16[4,1,128,1024]{2,3,1,0:T(8,128)(2,1)}), bf16[4,1,128,1024]{2,3,1,0:T(8,128)(2,1)S(1)}, u32[]{:S(2)}, u32[]{:S(2)}) async-start(bf16[4,1,128,1024]{2,3,1,0:T(8,128)(2,1)} %broadcast_in_dim.42), calls=%async_computation.1 | async-start | bytes 2097152 | tf_op jit(solution)/shard_map/all_to_all | solution.py:19
  116.7 26.5 %collective-permute-start.6 = (f32[128,128]{1,0:T(8,128)S(1)}, f32[128,128]{1,0:T(8,128)S(1)}, u32[]{:S(2)}, u32[]{:S(2)}) collective-permute-start(f32[128,128]{1,0:T(8,128)S(1)} %bitcast_convert_fusion), channel_id=1, source_target_pairs={{0,1},{1,0},{2,3},{3,2},{4,5},{5,4},{6,7},{7,6},{8,9},{9,8},{10,11... | collective-permute-start | bytes 196616 | tf_op jit(solution)/shard_map/ppermute | solution.py:14
  130.4 3.4 %copy-start.4 = (f32[128,1024]{1,0:T(8,128)S(1)}, f32[128,1024]{1,0:T(8,128)}, u32[]{:S(2)}) copy-start(f32[128,1024]{1,0:T(8,128)} %copy-done.3) | copy-start | bytes 1572868
  135.0 3.9 %copy-start.8 = (f32[128,1024]{1,0:T(8,128)S(1)}, f32[128,1024]{1,0:T(8,128)}, u32[]{:S(2)}) copy-start(f32[128,1024]{1,0:T(8,128)} %copy-done.7) | copy-start | bytes 1572868
  137.7 3.7 %copy-start.6 = (f32[128,1024]{0,1:T(8,128)S(1)}, f32[128,1024]{0,1:T(8,128)}, u32[]{:S(2)}) copy-start(f32[128,1024]{0,1:T(8,128)} %copy-done.5) | copy-start | bytes 1572868
  138.9 3.6 %copy-start.12 = (bf16[1,128,128]{2,1,0:T(8,128)(2,1)S(1)}, bf16[1,128,128]{2,1,0:T(8,128)(2,1)}, u32[]{:S(2)}) copy-start(bf16[1,128,128]{2,1,0:T(8,128)(2,1)} %param.24) | copy-start | bytes 98308
  140.1 3.0 %copy-start.2 = (f32[128,1024]{0,1:T(8,128)S(1)}, f32[128,1024]{0,1:T(8,128)}, u32[]{:S(2)}) copy-start(f32[128,1024]{0,1:T(8,128)} %copy-done.1) | copy-start | bytes 1572868
  160.5 5.4 %copy-start.13 = (pred[1024]{0:T(1024)(128)(4,1)S(1)}, pred[1024]{0:T(1024)(128)(4,1)}, u32[]{:S(2)}) copy-start(pred[1024]{0:T(1024)(128)(4,1)} %compare_and_fusion) | copy-start | bytes 3076
where the time goes:
time: 222 us; the launch traced here: 220 us
  waiting for transfers between devices  76.9 us (35%)
  blocking collectives  51.4 us (23%)
  matrix products  41.5 us (19%)
  local copies, waits for them, and re-layouts  21.2 us (10%)
  starting transfers between devices  21.1 us (10%)
  other arithmetic  7.26 us (3%)
    all_to_all x1, blocking collectives, redistribute(): lax.all_to_all(columns.reshape(devices, block_rows, slab_rows), ('grp', '...  51.4 us
    ppermute x7, waiting for transfers between devices, from_partner(): return lax.ppermute(block, axis, route)  45.7 us
    all_to_all x1, waiting for transfers between devices, redistribute(): lax.all_to_all(columns.reshape(devices, block_rows, slab_rows), ('grp', '...  29.8 us
    dot_general x23, matrix products, transform(): jnp.dot(matrix.astype(jnp.float32), stacked, precision=lax.Precision.HIGH...  27.1 us
    all_to_all x1, starting transfers between devices, redistribute(): lax.all_to_all(columns.reshape(devices, block_rows, slab_rows), ('grp', '...  11.5 us
    dot_general x4, matrix products, one_tile(): jnp.dot(out_rows, incoming_b, preferred_element_type=jnp.float32)  6.75 us
    ppermute x7, starting transfers between devices, from_partner(): return lax.ppermute(block, axis, route)  6.1 us
    dot_general x4, matrix products, one_tile(): jnp.dot(diag_rows, masked, preferred_element_type=jnp.float32)  5.55 us
  transfers between devices with their start and end apart: 9, of which 7 were waited for; matrix products, arithmetic and copies ran while one was open for 12% of the time, Pallas kernels for 0%

commit v1 on v0

v1 whole, which is shorter than its diff:
```python
import functools

import jax
import jax.numpy as jnp
from jax import lax
from jax.experimental import pallas as pl
from jax.experimental.pallas import tpu as pltpu
from jax.sharding import PartitionSpec as P

BOTH = ("grp", "leaf")
NT = (((1,), (1,)), ((), ()))
TN = (((0,), (0,)), ((), ()))


def exchange(blocks):
    return lax.all_to_all(blocks, BOTH, split_axis=0, concat_axis=0, tiled=True)


def dot(a, b, dims):
    return lax.dot_general(a, b, dims, preferred_element_type=jnp.float32)


def split_rows(value):
    head = value.astype(jnp.bfloat16).astype(jnp.float32)
    return jnp.concatenate([head, value - head], axis=0).astype(jnp.bfloat16)


def times_transposed(pair, matrix):
    both = dot(pair, matrix, NT)
    rows = both.shape[0] // 2
    return both[:rows] + both[rows:]


def tree_kernel(
    levels, parts_ref, lift_hbm, couple_hbm, spread_hbm, out_ref, lift, couple, spread, cross, sems
):
    copies = {}
    inner = levels - 1
    slot = 0

    def fetch(name, source, target, start, size):
        nonlocal slot
        copy = pltpu.make_async_copy(
            source.at[pl.ds(start, size)], target.at[pl.ds(start, size)], sems.at[slot]
        )
        copy.start()
        copies[name] = copy
        slot += 1

    for height in range(1, levels):
        nodes = 1 << (levels - height)
        if height < inner:
            fetch(("lift", height), lift_hbm, lift, nodes - 4, nodes)
        fetch(("couple", height), couple_hbm, couple, nodes - 2, nodes)
    for height in range(inner - 1, 0, -1):
        nodes = 1 << (levels - height)
        fetch(("spread", height), spread_hbm, spread, nodes - 4, nodes)

    count = 1 << inner
    skeletons = [
        parts_ref[2 * n].astype(jnp.float32) + parts_ref[2 * n + 1].astype(jnp.float32)
        for n in range(count)
    ]
    for height in range(1, levels):
        nodes = 1 << (levels - height)
        if height < inner:
            copies["lift", height].wait()
        copies["couple", height].wait()
        lifted = []
        for n in range(nodes):
            pair = split_rows(skeletons[n])
            cross[nodes - 2 + (n ^ 1)] = times_transposed(pair, couple[nodes - 2 + n])
            if height < inner:
                lifted.append(times_transposed(pair, lift[nodes - 4 + n]))
        skeletons = [lifted[n] + lifted[n + 1] for n in range(0, len(lifted), 2)]
    incoming = [cross[0], cross[1]]
    for height in range(inner - 1, 0, -1):
        nodes = 1 << (levels - height)
        copies["spread", height].wait()
        below = []
        for parent in range(nodes // 2):
            pair = split_rows(incoming[parent])
            for child in (2 * parent, 2 * parent + 1):
                below.append(
                    times_transposed(pair, spread[nodes - 4 + child]) + cross[nodes - 2 + child]
                )
        incoming = below
    for n in range(count):
        value = incoming[n].astype(out_ref.dtype)
        out_ref[2 * n] = value
        out_ref[2 * n + 1] = value


def tree(parts, inner_lift, inner_couple, inner_spread):
    devices, width, rank = parts.shape
    levels = devices.bit_length() - 1
    anywhere = pl.BlockSpec(memory_space=pl.ANY)
    inside = pl.BlockSpec(memory_space=pltpu.VMEM)
    return pl.pallas_call(
        functools.partial(tree_kernel, levels),
        out_shape=jax.ShapeDtypeStruct(parts.shape, jnp.bfloat16),
        in_specs=[inside, anywhere, anywhere, anywhere],
        out_specs=inside,
        scratch_shapes=[
            pltpu.VMEM(inner_lift.shape, jnp.bfloat16),
            pltpu.VMEM(inner_couple.shape, jnp.bfloat16),
            pltpu.VMEM(inner_spread.shape, jnp.bfloat16),
            pltpu.VMEM((inner_couple.shape[0], width, rank), jnp.float32),
            pltpu.SemaphoreType.DMA((3 * levels,)),
        ],
        compiler_params=pltpu.CompilerParams(vmem_limit_bytes=24 << 20),
        cost_estimate=pl.CostEstimate(
            flops=4 * 374 * 16 * 128 * 128, bytes_accessed=13 << 20, transcendentals=0
        ),
        name="tree",
    )(parts, inner_lift, inner_couple, inner_spread)


def local(
    basis_slab,
    live_counts,
    pole_order,
    leaf_diag,
    leaf_in,
    leaf_out,
    leaf_lift,
    leaf_couple,
    leaf_spread,
    inner_lift,
    inner_couple,
    inner_spread,
):
    devices = lax.axis_size("grp") * lax.axis_size("leaf")
    width, columns = basis_slab.shape
    rank = leaf_in.shape[1]
    block_rows = width // devices
    owned = columns // devices

    poles = exchange(basis_slab.reshape(devices, block_rows, columns)).reshape(width, columns)

    index = jnp.arange(width, dtype=jnp.int32)
    slot_pole = jnp.where(index < live_counts[0], pole_order[0], -1)
    select = (slot_pole[:, None] == index[None, :]).astype(jnp.bfloat16)
    is_live = jnp.any(slot_pole[:, None] == index[None, :], axis=0)
    generators = dot(select, jnp.concatenate([leaf_in, leaf_out], axis=1), TN).astype(jnp.bfloat16)
    in_poles, out_poles = generators[:, :rank], generators[:, rank:]
    rows = dot(select, leaf_diag, TN).astype(jnp.bfloat16)
    diag = dot(rows, select, (((1,), (0,)), ((), ())))
    dead_diag = (index[:, None] == index[None, :]) & ~is_live[:, None]
    diag = jnp.where(dead_diag, 1.0, diag).astype(jnp.bfloat16)

    skeleton = dot(poles, in_poles, TN)
    pair = split_rows(skeleton)
    lifted = times_transposed(pair, leaf_lift[0]).astype(jnp.bfloat16)
    coupled = times_transposed(pair, leaf_couple[0]).astype(jnp.bfloat16)
    leaves = lax.axis_size("leaf")
    cross = lax.ppermute(coupled, "leaf", [(i, i ^ 1) for i in range(leaves)])
    parts = exchange(lifted.reshape(devices, owned, rank))
    near = dot(diag, poles, (((1,), (0,)), ((), ())))
    above = exchange(tree(parts, inner_lift, inner_couple, inner_spread))
    incoming = dot(above.reshape(columns, rank), leaf_spread[0], NT) + cross.astype(jnp.float32)
    updated = near + dot(out_poles, incoming.astype(jnp.bfloat16), NT)
    merged = exchange(updated.astype(jnp.bfloat16).reshape(devices, block_rows, columns))
    return merged.reshape(width, columns)


def solution(mesh):
    placed = (
        P(BOTH, None),
        P(BOTH),
        P(BOTH, None),
        P(BOTH, None),
        P(BOTH, None),
        P(BOTH, None),
        P(BOTH, None, None),
        P(BOTH, None, None),
        P(BOTH, None, None),
        P(),
        P(),
        P(),
    )
    return jax.shard_map(
        local, mesh=mesh, in_specs=placed, out_specs=P(BOTH, None), check_vma=False
    )
```

time: 222 us -> 135 us (0.61)
  waiting for transfers between devices: 76.9 us -> 34.7 us
  matrix products: 41.5 us -> 21.1 us
  blocking collectives: 51.4 us -> 35.7 us
  local copies, waits for them, and re-layouts: 21.2 us -> 7.82 us
  Pallas kernels: 0 us -> 9.97 us
  other arithmetic: 7.26 us -> 2.14 us
    ppermute x7 -> x1, waiting for transfers between devices: 45.7 us -> 0.01 us  [local(): cross = lax.ppermute(coupled, 'leaf', [(i, i ^ 1) for i in range(leaves)])]
    dot_general x33 -> x7, matrix products: 41.5 us -> 21.1 us  [dot(): return lax.dot_general(a, b, dims, preferred_element_type=jnp.float32)]
    all_to_all x1, blocking collectives: 51.4 us -> 35.7 us  [exchange(): return lax.all_to_all(blocks, BOTH, split_axis=0, concat_axis=0, tiled=True)]
    gather x2 -> x0, local copies, waits for them, and re-layouts: 10.7 us -> none  [the longest x1 5.34 us: local(): restored = jnp.take(updated, inverse, axis=0)]
    pallas_call x0 -> x1, Pallas kernels: none -> 9.97 us  [tree(): pl.pallas_call(functools.partial(tree_kernel, levels), out_shape=jax.Shap...]
    all_to_all x2 -> x3, starting transfers between devices: 15 us -> 20.7 us  [exchange(): return lax.all_to_all(blocks, BOTH, split_axis=0, concat_axis=0, tiled=True)]
    unnamed x29 -> x21, local copies, waits for them, and re-layouts: 2.18 us -> 7.82 us
    ppermute x7 -> x1, starting transfers between devices: 6.1 us -> 1.21 us  [local(): cross = lax.ppermute(coupled, 'leaf', [(i, i ^ 1) for i in range(leaves)])]
  transfers between devices with their start and end apart: 9 -> 4, of which waited for: 7 -> 3; matrix products, arithmetic and copies ran while one was open for 12% -> 12% of each run, Pallas kernels for 0% -> 7%
where the time goes in v1:
time: 135 us; the launch traced here: 134 us
  blocking collectives  35.7 us (26%)
  waiting for transfers between devices  34.7 us (26%)
  starting transfers between devices  21.9 us (16%)
  matrix products  21.1 us (16%)
  Pallas kernels  9.97 us (7%)
  local copies, waits for them, and re-layouts  7.82 us (6%)
  other arithmetic  2.14 us (2%)
    all_to_all x1, blocking collectives, exchange(): return lax.all_to_all(blocks, BOTH, split_axis=0, concat_axis=0, tiled=True)  35.7 us
    all_to_all x3, waiting for transfers between devices, exchange(): return lax.all_to_all(blocks, BOTH, split_axis=0, concat_axis=0, tiled=True)  34.7 us
    dot_general x7, matrix products, dot(): return lax.dot_general(a, b, dims, preferred_element_type=jnp.float32)  21.1 us
    all_to_all x3, starting transfers between devices, exchange(): return lax.all_to_all(blocks, BOTH, split_axis=0, concat_axis=0, tiled=True)  20.7 us
    pallas_call x1, Pallas kernels, tree(): pl.pallas_call(functools.partial(tree_kernel, levels), out_shape=jax.Shap...  9.97 us
    unnamed x21, local copies, waits for them, and re-layouts  7.82 us
  transfers between devices with their start and end apart: 4, of which 3 were waited for; matrix products, arithmetic and copies ran while one was open for 12% of the time, Pallas kernels for 7%

profile of v1, /device:TPU:1, one launch (start us, length us, event | category | flops | bytes accessed | tf_op | source)
XLA Modules:
  0.0 134.3 jit_solution(10334380271008833261)
XLA Ops:
  0.0 12.0 %all-to-all-start = ((bf16[128,8,1024]{2,1,0:T(8,128)(2,1)}), bf16[128,8,1024]{2,1,0:T(8,128)(2,1)}, u32[]{:S(2)}, u32[]{:S(2)}) async-start(bf16[128,8,1024]{2,1,0:T(8,128)(2,1)} %bitcast.39), calls=%async_computation | async-start | bytes 4194304 | tf_op jit(solution)/shard_map/all_to_all | solution.py:16
  12.6 0.6 fusion.3
  13.3 1.4 %fusion.16 = bf16[1024,256]{1,0:T(8,128)(2,1)S(1)} fusion(s32[1024]{0:T(1024)S(1)} %fusion.40, bf16[1024,128]{1,0:T(8,128)(2,1)S(1)} %copy-done.8, bf16[1024,128]{1,0:T(8,128)(2,1)S(1)} %copy-done.9), kind=kOutput, calls=%fused_computation.20 | convolution fusion | flops 539230208 | bytes 1052672 | tf_op jit(solution)/shard_map/dot_general | solution.py:20
  14.7 6.0 %fusion.1 = bf16[1024,1024]{1,0:T(8,128)(2,1)} fusion(s32[1024]{0:T(1024)S(1)} %fusion.40, bf16[1024,1024]{1,0:T(8,128)(2,1)S(1)} %copy-done), kind=kOutput, calls=%fused_computation.4 | convolution fusion | flops 4298113024 | bytes 4198400 | tf_op jit(solution)/shard_map/dot_general | solution.py:20
  20.8 21.3 %all-to-all-done = bf16[128,8,1024]{2,1,0:T(8,128)(2,1)} async-done(((bf16[128,8,1024]{2,1,0:T(8,128)(2,1)}), bf16[128,8,1024]{2,1,0:T(8,128)(2,1)}, u32[]{:S(2)}, u32[]{:S(2)}) %all-to-all-start) | async-done | bytes 2097184 | tf_op jit(solution)/shard_map/all_to_all | solution.py:16
  42.1 2.1 %fusion.45 = (bf16[1024,128]{0,1:T(8,128)(2,1)S(1)}, bf16[1024,128]{0,1:T(8,128)(2,1)S(1)}) fusion(bf16[128,8,1024]{2,1,0:T(8,128)(2,1)} %all-to-all-done, bf16[1024,256]{1,0:T(8,128)(2,1)S(1)} %fusion.16), kind=kOutput, calls=%fused_computation.48 | convolution fusion | flops 268959744 | bytes 2883584 | tf_op jit(solution)/shard_map/dot_general | solution.py:20
  44.2 0.0 copy-start.6
  44.2 0.3 fusion.26
  44.5 0.8 fusion.27
  45.3 4.4 %all-to-all-start.1 = ((bf16[128,8,128]{2,1,0:T(8,128)(2,1)}), bf16[128,8,128]{2,1,0:T(8,128)(2,1)S(1)}, u32[]{:S(2)}, u32[]{:S(2)}) async-start(bf16[128,8,128]{2,1,0:T(8,128)(2,1)} %fusion.27), calls=%async_computation.1 | async-start | bytes 524288 | tf_op jit(solution)/shard_map/all_to_all | solution.py:16
  49.6 0.3 fusion.25
  50.0 0.8 fusion.20
  50.7 1.2 collective-permute-start
  51.9 8.9 %all-to-all-done.1.parts_ref = bf16[128,8,128]{2,1,0:T(8,128)(2,1)S(1)} async-done(((bf16[128,8,128]{2,1,0:T(8,128)(2,1)}), bf16[128,8,128]{2,1,0:T(8,128)(2,1)S(1)}, u32[]{:S(2)}, u32[]{:S(2)}) %all-to-all-start.1) | async-done | bytes 262176 | tf_op jit(solution)/shard_map/all_to_all | solution.py:16
  60.8 2.2 %copy-done.1 = bf16[126,128,128]{2,1,0:T(8,128)(2,1)S(1)} copy-done((bf16[126,128,128]{2,1,0:T(8,128)(2,1)S(1)}, bf16[126,128,128]{2,1,0:T(8,128)(2,1)}, u32[]{:S(2)}) %copy-start.1) | copy-done | bytes 4128792
  63.0 2.1 %copy-done.2 = bf16[124,128,128]{2,1,0:T(8,128)(2,1)S(1)} copy-done((bf16[124,128,128]{2,1,0:T(8,128)(2,1)S(1)}, bf16[124,128,128]{2,1,0:T(8,128)(2,1)}, u32[]{:S(2)}) %copy-start.2) | copy-done | bytes 4063256
  65.2 2.1 %copy-done.3 = bf16[124,128,128]{2,1,0:T(8,128)(2,1)S(1)} copy-done((bf16[124,128,128]{2,1,0:T(8,128)(2,1)S(1)}, bf16[124,128,128]{2,1,0:T(8,128)(2,1)}, u32[]{:S(2)}) %copy-start.3) | copy-done | bytes 4063256
  67.3 10.0 %tree.1 = bf16[128,8,128]{2,1,0:T(8,128)(2,1)} custom-call(bf16[128,8,128]{2,1,0:T(8,128)(2,1)S(1)} %all-to-all-done.1.parts_ref, bf16[124,128,128]{2,1,0:T(8,128)(2,1)S(1)} %copy-done.2, bf16[126,128,128]{2,1,0:T(8,128)(2,1)S(1)} %copy-done.1, bf16[124,128,128]{2,1,0:T(8,128)(2,1)S(1)} %copy-done.3), custom_call_target="tpu_custom_call" | custom-call | flops 392167424 | bytes 13631488 | tf_op jit(solution)/shard_map/tree/pallas_call | solution.py:99
  77.3 4.4 %all-to-all-start.2 = ((bf16[128,8,128]{2,1,0:T(8,128)(2,1)}), bf16[128,8,128]{2,1,0:T(8,128)(2,1)S(1)}, u32[]{:S(2)}, u32[]{:S(2)}) async-start(bf16[128,8,128]{2,1,0:T(8,128)(2,1)} %tree.1), calls=%async_computation.2 | async-start | bytes 524288 | tf_op jit(solution)/shard_map/all_to_all | solution.py:16
  81.7 6.6 %fusion.5 = f32[1024,1024]{1,0:T(8,128)} fusion(bf16[1024,1024]{1,0:T(8,128)(2,1)} %fusion.1, bf16[128,8,1024]{2,1,0:T(8,128)(2,1)} %all-to-all-done, pred[1024]{0:T(1024)(128)(4,1)S(1)} %not.8), kind=kOutput, calls=%fused_computation.9 | convolution fusion | flops 2150629376 | bytes 8389632 | tf_op jit(solution)/shard_map/dot_general | solution.py:20
  88.3 4.5 %all-to-all-done.2 = bf16[128,8,128]{2,1,0:T(8,128)(2,1)S(1)} async-done(((bf16[128,8,128]{2,1,0:T(8,128)(2,1)}), bf16[128,8,128]{2,1,0:T(8,128)(2,1)S(1)}, u32[]{:S(2)}, u32[]{:S(2)}) %all-to-all-start.2) | async-done | bytes 262176 | tf_op jit(solution)/shard_map/all_to_all | solution.py:16
  92.8 4.4 %fusion.15 = bf16[128,8,1024]{2,1,0:T(8,128)(2,1)} fusion(f32[1024,1024]{1,0:T(8,128)} %fusion.5, bf16[1024,128]{1,0:T(8,128)(2,1)S(1)} %collective-permute-done, bf16[1024,256]{1,0:T(8,128)(2,1)S(1)} %fusion.16, bf16[128,8,128]{2,1,0:T(8,128)(2,1)S(1)} %all-to-all-done.2, bf16[1,128,128]{2,1,0:T(8,128)(2,1)S(1)} %copy-done.4), kind=kOutput, calls=%fused_computation.19 | convolution fusion | flops 304480256 | bytes 7110656 | tf_op jit(solution)/shard_map/dot_general | solution.py:20
  97.2 35.7 %all_to_all.20 = bf16[128,8,1024]{2,1,0:T(8,128)(2,1)S(1)} all-to-all(bf16[128,8,1024]{2,1,0:T(8,128)(2,1)} %fusion.15), channel_id=1, replica_groups=mesh['grp'=4,'leaf'=32] {'grp','leaf'}, dimensions={0} | all-to-all | bytes 4194304 | tf_op jit(solution)/shard_map/all_to_all | solution.py:16
  133.0 1.3 copy.15
  (19 shorter events, 0.0 us)
Async XLA Ops:
  0.0 14.7 %copy-start = (bf16[1024,1024]{1,0:T(8,128)(2,1)S(1)}, bf16[1024,1024]{1,0:T(8,128)(2,1)}, u32[]{:S(2)}) copy-start(bf16[1024,1024]{1,0:T(8,128)(2,1)} %param.15) | copy-start | bytes 6291460
  0.0 12.6 %copy-start.7 = (s32[1,1024]{1,0:T(1,128)S(1)}, s32[1,1024]{1,0:T(1,128)}, u32[]{:S(2)}) copy-start(s32[1,1024]{1,0:T(1,128)} %param.14) | copy-start | bytes 12292
  0.0 13.3 %copy-start.8 = (bf16[1024,128]{1,0:T(8,128)(2,1)S(1)}, bf16[1024,128]{1,0:T(8,128)(2,1)}, u32[]{:S(2)}) copy-start(bf16[1024,128]{1,0:T(8,128)(2,1)} %param.17) | copy-start | bytes 786436
  0.0 13.3 %copy-start.9 = (bf16[1024,128]{1,0:T(8,128)(2,1)S(1)}, bf16[1024,128]{1,0:T(8,128)(2,1)}, u32[]{:S(2)}) copy-start(bf16[1024,128]{1,0:T(8,128)(2,1)} %param.16) | copy-start | bytes 786436
  0.0 42.1 %all-to-all-start = ((bf16[128,8,1024]{2,1,0:T(8,128)(2,1)}), bf16[128,8,1024]{2,1,0:T(8,128)(2,1)}, u32[]{:S(2)}, u32[]{:S(2)}) async-start(bf16[128,8,1024]{2,1,0:T(8,128)(2,1)} %bitcast.39), calls=%async_computation | async-start | bytes 4194304 | tf_op jit(solution)/shard_map/all_to_all | solution.py:16
  20.8 23.4 %copy-start.5 = (bf16[1,128,128]{2,1,0:T(8,128)(2,1)S(1)}, bf16[1,128,128]{2,1,0:T(8,128)(2,1)}, u32[]{:S(2)}) copy-start(bf16[1,128,128]{2,1,0:T(8,128)(2,1)} %param.18) | copy-start | bytes 98308
  44.2 5.5 %copy-start.6 = (bf16[1,128,128]{2,1,0:T(8,128)(2,1)S(1)}, bf16[1,128,128]{2,1,0:T(8,128)(2,1)}, u32[]{:S(2)}) copy-start(bf16[1,128,128]{2,1,0:T(8,128)(2,1)} %param.19) | copy-start | bytes 98308
  45.3 15.6 %all-to-all-start.1 = ((bf16[128,8,128]{2,1,0:T(8,128)(2,1)}), bf16[128,8,128]{2,1,0:T(8,128)(2,1)S(1)}, u32[]{:S(2)}, u32[]{:S(2)}) async-start(bf16[128,8,128]{2,1,0:T(8,128)(2,1)} %fusion.27), calls=%async_computation.1 | async-start | bytes 524288 | tf_op jit(solution)/shard_map/all_to_all | solution.py:16
  50.7 37.6 %collective-permute-start = (bf16[1024,128]{1,0:T(8,128)(2,1)}, bf16[1024,128]{1,0:T(8,128)(2,1)S(1)}, u32[]{:S(2)}, u32[]{:S(2)}) collective-permute-start(bf16[1024,128]{1,0:T(8,128)(2,1)} %fusion.20), channel_id=1, source_target_pairs={{0,1},{1,0},{2,3},{3,2},{4,5},{5,4},{6,7},{7,6},{8,9},{9,8},{10,11... | collective-permute-start | bytes 786440 | tf_op jit(solution)/shard_map/ppermute | solution.py:157
  60.8 2.2 %copy-start.1 = (bf16[126,128,128]{2,1,0:T(8,128)(2,1)S(1)}, bf16[126,128,128]{2,1,0:T(8,128)(2,1)}, u32[]{:S(2)}) copy-start(bf16[126,128,128]{2,1,0:T(8,128)(2,1)} %couple_hbm.1) | copy-start | bytes 12386308
  63.0 2.2 %copy-start.2 = (bf16[124,128,128]{2,1,0:T(8,128)(2,1)S(1)}, bf16[124,128,128]{2,1,0:T(8,128)(2,1)}, u32[]{:S(2)}) copy-start(bf16[124,128,128]{2,1,0:T(8,128)(2,1)} %lift_hbm.1) | copy-start | bytes 12189700
  65.2 2.2 %copy-start.3 = (bf16[124,128,128]{2,1,0:T(8,128)(2,1)S(1)}, bf16[124,128,128]{2,1,0:T(8,128)(2,1)}, u32[]{:S(2)}) copy-start(bf16[124,128,128]{2,1,0:T(8,128)(2,1)} %spread_hbm.1) | copy-start | bytes 12189700
  77.3 15.5 %all-to-all-start.2 = ((bf16[128,8,128]{2,1,0:T(8,128)(2,1)}), bf16[128,8,128]{2,1,0:T(8,128)(2,1)S(1)}, u32[]{:S(2)}, u32[]{:S(2)}) async-start(bf16[128,8,128]{2,1,0:T(8,128)(2,1)} %tree.1), calls=%async_computation.2 | async-start | bytes 524288 | tf_op jit(solution)/shard_map/all_to_all | solution.py:16
  81.7 11.1 %copy-start.4 = (bf16[1,128,128]{2,1,0:T(8,128)(2,1)S(1)}, bf16[1,128,128]{2,1,0:T(8,128)(2,1)}, u32[]{:S(2)}) copy-start(bf16[1,128,128]{2,1,0:T(8,128)(2,1)} %param.20) | copy-start | bytes 98308

commit v2 on v1

v2 whole, which is shorter than its diff:
```python
import functools

import jax
import jax.numpy as jnp
from jax import lax
from jax.experimental import pallas as pl
from jax.experimental.pallas import tpu as pltpu
from jax.sharding import PartitionSpec as P

BOTH = ("grp", "leaf")
NN = (((1,), (0,)), ((), ()))
NT = (((1,), (1,)), ((), ()))
TN = (((0,), (0,)), ((), ()))


def exchange(blocks):
    return lax.all_to_all(blocks, BOTH, split_axis=0, concat_axis=0, tiled=True)


def dot(a, b, dims):
    return lax.dot_general(a, b, dims, preferred_element_type=jnp.float32)


def split_rows(value):
    head = value.astype(jnp.bfloat16).astype(jnp.float32)
    return jnp.concatenate([head, value - head], axis=0).astype(jnp.bfloat16)


def kernel_options(mebibytes):
    return pltpu.CompilerParams(vmem_limit_bytes=mebibytes << 20)


def cost(flops, moved):
    return pl.CostEstimate(flops=flops, bytes_accessed=moved, transcendentals=0)


FAR = pl.BlockSpec(memory_space=pltpu.HBM)
INSIDE = pl.BlockSpec(memory_space=pltpu.VMEM)
TILE = 256


def fold_kernel(
    slot_ref, diag_hbm, both_ref, in_ref, out_ref, spread_ref,
    in_both_ref, out_poles_ref, out_spread_ref, folded_hbm,
    chosen, diag, folded, sems,
):
    width = diag.shape[0]
    load = pltpu.make_async_copy(diag_hbm, diag, sems.at[0])
    load.start()
    slots = slot_ref[...]
    for low in range(0, width, TILE):
        pole = lax.broadcasted_iota(jnp.int32, (TILE, width), 0) + low
        chosen[pl.ds(low, TILE)] = jnp.where(pole == slots, 1.0, 0.0).astype(jnp.bfloat16)
    in_poles = dot(chosen[...], in_ref[...], NN).astype(jnp.bfloat16)
    in_both_ref[...] = dot(both_ref[...], in_poles, NT).astype(jnp.bfloat16)
    out_poles = dot(chosen[...], out_ref[...], NN).astype(jnp.bfloat16)
    out_poles_ref[...] = out_poles
    out_spread_ref[...] = dot(out_poles, spread_ref[...], NN).astype(jnp.bfloat16)
    load.wait()
    stores = []
    for number, low in enumerate(range(0, width, TILE)):
        piece = pl.ds(low, TILE)
        rows = dot(chosen[piece], diag[...], NN).astype(jnp.bfloat16)
        value = dot(rows, chosen[...], NT)
        pole = lax.broadcasted_iota(jnp.int32, (TILE, width), 0) + low
        other = lax.broadcasted_iota(jnp.int32, (TILE, width), 1)
        live = jnp.sum(chosen[piece].astype(jnp.float32), axis=1, keepdims=True)
        value = jnp.where((pole == other) & (live < 0.5), 1.0, value)
        folded[piece] = value.astype(jnp.bfloat16)
        store = pltpu.make_async_copy(
            folded.at[piece], folded_hbm.at[piece], sems.at[1 + number]
        )
        store.start()
        stores.append(store)
    for store in stores:
        store.wait()


def fold(slot_pole, leaf_diag, both, leaf_in, leaf_out, spread):
    width = leaf_diag.shape[0]
    rank = leaf_in.shape[1]
    square = pltpu.VMEM((width, width), jnp.bfloat16)
    tall = jax.ShapeDtypeStruct((width, rank), jnp.bfloat16)
    return pl.pallas_call(
        fold_kernel,
        out_shape=(
            jax.ShapeDtypeStruct((2 * rank, width), jnp.bfloat16),
            tall,
            tall,
            pltpu.HBM((width, width), jnp.bfloat16),
        ),
        in_specs=[INSIDE, FAR, INSIDE, INSIDE, INSIDE, INSIDE],
        out_specs=(INSIDE, INSIDE, INSIDE, FAR),
        scratch_shapes=[square, square, square, pltpu.SemaphoreType.DMA((1 + width // TILE,))],
        compiler_params=kernel_options(32),
        cost_estimate=cost(5 * width**3, 6 << 20),
        name="fold",
    )(slot_pole, in_hbm(leaf_diag), both, leaf_in, leaf_out, spread)


def rise_kernel(rows_ref, poles_ref, lifted_ref, coupled_ref):
    rank = lifted_ref.shape[1]
    for low in range(0, poles_ref.shape[1], TILE):
        value = dot(rows_ref[...], poles_ref[:, pl.ds(low, TILE)], NN)
        value = value.T.astype(jnp.bfloat16)
        lifted_ref[pl.ds(low, TILE)] = value[:, :rank]
        coupled_ref[pl.ds(low, TILE)] = value[:, rank:]


def rise(rows, poles, rank):
    width, columns = poles.shape
    out = jax.ShapeDtypeStruct((columns, rank), jnp.bfloat16)
    return pl.pallas_call(
        rise_kernel,
        out_shape=(out, out),
        in_specs=[INSIDE, INSIDE],
        out_specs=(INSIDE, INSIDE),
        compiler_params=kernel_options(16),
        cost_estimate=cost(2 * rows.shape[0] * width * columns, 3 << 20),
        name="rise",
    )(rows, poles)


def in_hbm(array):
    return pltpu.with_memory_space_constraint(array, pltpu.HBM)


def tree_kernel(
    levels, parts_ref, lift_hbm, couple_hbm, spread_hbm, out_ref, lift, couple, spread, cross, sems
):
    inner = levels - 1
    count = 1 << inner
    rank = parts_ref.shape[2]
    copies = {}
    number = 0

    def fetch(first, source, target, offset, start, stop):
        nonlocal number
        piece = pl.ds(start - offset, stop - start)
        copy = pltpu.make_async_copy(source.at[piece], target.at[piece], sems.at[number])
        copy.start()
        copies.setdefault(first, []).append(copy)
        number += 1

    half, quarter, middle = count // 2, count // 4, count + count // 2
    for first, start, stop in (
        (count, count, middle),
        (middle, middle, 2 * count),
        (half, half, count),
        (quarter, 2, half),
    ):
        fetch(("up", first), lift_hbm, lift, 4, max(start, 4), stop)
        fetch(("up", first), couple_hbm, couple, 2, start, stop)
    for start, stop in ((4, half), (half, count), (count, 2 * count)):
        fetch(("down", start), spread_hbm, spread, 4, start, stop)

    def arrived(way, node):
        for copy in copies.get((way, node), ()):
            copy.wait()

    def apart(first, second):
        first, second = split_rows(first), split_rows(second)
        blank = jnp.zeros_like(first)
        return jnp.concatenate(
            [
                jnp.concatenate([first, blank], axis=1),
                jnp.concatenate([blank, second], axis=1),
            ],
            axis=0,
        )

    def beside(first, second):
        return jnp.concatenate([first, second], axis=1)

    width = parts_ref.shape[1]

    def joined(rows):
        return rows[:width] + rows[width:]

    skeletons = {
        count + n: parts_ref[2 * n].astype(jnp.float32) + parts_ref[2 * n + 1].astype(jnp.float32)
        for n in range(count)
    }
    for height in range(1, levels):
        nodes = 1 << (levels - height)
        for node in range(nodes, 2 * nodes, 2):
            arrived("up", node)
            pair = apart(skeletons[node], skeletons[node + 1])
            couples = beside(couple[node - 2], couple[node - 1])
            if height < inner:
                lifts = beside(lift[node - 4], lift[node - 3])
                both = dot(pair, jnp.concatenate([lifts, couples], axis=0), NT)
                up, across = both[:, :rank], both[:, rank:]
                skeletons[node // 2] = joined(up[: 2 * width] + up[2 * width :])
            else:
                across = dot(pair, couples, NT)
            cross[node - 1] = joined(across[: 2 * width])
            cross[node - 2] = joined(across[2 * width :])
    incoming = {2: cross[0], 3: cross[1]}
    for height in range(inner - 1, 0, -1):
        nodes = 1 << (levels - height)
        for node in range(nodes, 2 * nodes, 4):
            arrived("down", node)
            pair = apart(incoming[node // 2], incoming[node // 2 + 1])
            matrices = jnp.concatenate(
                [
                    beside(spread[node - 4], spread[node - 2]),
                    beside(spread[node - 3], spread[node - 1]),
                ],
                axis=0,
            )
            both = dot(pair, matrices, NT)
            for child in range(4):
                rows = both[2 * width * (child // 2) :][: 2 * width]
                value = joined(rows[:, rank * (child % 2) :][:, :rank])
                incoming[node + child] = value + cross[node + child - 2]
    for n in range(count):
        value = incoming[count + n].astype(out_ref.dtype)
        out_ref[2 * n] = value
        out_ref[2 * n + 1] = value


def tree(parts, inner_lift, inner_couple, inner_spread):
    devices, width, rank = parts.shape
    levels = devices.bit_length() - 1
    return pl.pallas_call(
        functools.partial(tree_kernel, levels),
        out_shape=jax.ShapeDtypeStruct(parts.shape, jnp.bfloat16),
        in_specs=[INSIDE, FAR, FAR, FAR],
        out_specs=INSIDE,
        scratch_shapes=[
            pltpu.VMEM(inner_lift.shape, jnp.bfloat16),
            pltpu.VMEM(inner_couple.shape, jnp.bfloat16),
            pltpu.VMEM(inner_spread.shape, jnp.bfloat16),
            pltpu.VMEM((inner_couple.shape[0], width, rank), jnp.float32),
            pltpu.SemaphoreType.DMA((11,)),
        ],
        compiler_params=kernel_options(20),
        cost_estimate=cost(4 * 374 * 16 * 128 * 128, 13 << 20),
        name="tree",
    )(parts, in_hbm(inner_lift), in_hbm(inner_couple), in_hbm(inner_spread))


def near_kernel(diag_hbm, poles_hbm, out_poles_ref, cross_ref, near_ref, diag, poles, sems):
    width = diag.shape[0]
    whole = pltpu.make_async_copy(poles_hbm, poles, sems.at[width // TILE])
    whole.start()
    loads = []
    for number, low in enumerate(range(0, width, TILE)):
        piece = pl.ds(low, TILE)
        load = pltpu.make_async_copy(diag_hbm.at[piece], diag.at[piece], sems.at[number])
        load.start()
        loads.append(load)
    whole.wait()
    for number, low in enumerate(range(0, width, TILE)):
        piece = pl.ds(low, TILE)
        loads[number].wait()
        value = dot(diag[piece], poles[...], NN)
        value += dot(out_poles_ref[piece], cross_ref[...], NT)
        near_ref[piece] = value.astype(near_ref.dtype)


def near_field(diag, poles, out_poles, cross):
    width, columns = poles.shape
    rank = out_poles.shape[1]
    return pl.pallas_call(
        near_kernel,
        out_shape=jax.ShapeDtypeStruct((width, columns), jnp.bfloat16),
        in_specs=[FAR, FAR, INSIDE, INSIDE],
        out_specs=INSIDE,
        scratch_shapes=[
            pltpu.VMEM(diag.shape, jnp.bfloat16),
            pltpu.VMEM(poles.shape, jnp.bfloat16),
            pltpu.SemaphoreType.DMA((1 + width // TILE,)),
        ],
        compiler_params=kernel_options(24),
        cost_estimate=cost(2 * width * (width + rank) * columns, 7 << 20),
        name="near",
    )(in_hbm(diag), in_hbm(poles), out_poles, cross)


def fall_kernel(near_ref, out_spread_ref, above_ref, out_ref):
    for low in range(0, near_ref.shape[0], TILE):
        piece = pl.ds(low, TILE)
        far = dot(out_spread_ref[piece], above_ref[...], NT)
        out_ref[piece] = (near_ref[piece].astype(jnp.float32) + far).astype(out_ref.dtype)


def fall(near, out_spread, above):
    width, columns = near.shape
    rank = above.shape[1]
    return pl.pallas_call(
        fall_kernel,
        out_shape=jax.ShapeDtypeStruct((width, columns), jnp.bfloat16),
        in_specs=[INSIDE, INSIDE, INSIDE],
        out_specs=INSIDE,
        compiler_params=kernel_options(16),
        cost_estimate=cost(2 * width * rank * columns, 5 << 20),
        name="fall",
    )(near, out_spread, above)


def local(
    basis_slab,
    live_counts,
    pole_order,
    leaf_diag,
    leaf_in,
    leaf_out,
    leaf_lift,
    leaf_couple,
    leaf_spread,
    inner_lift,
    inner_couple,
    inner_spread,
):
    leaves = lax.axis_size("leaf")
    devices = lax.axis_size("grp") * leaves
    width, columns = basis_slab.shape
    rank = leaf_in.shape[1]
    block_rows = width // devices
    owned = columns // devices

    poles = exchange(basis_slab.reshape(devices, block_rows, columns)).reshape(width, columns)

    slot = lax.broadcasted_iota(jnp.int32, (1, width), 1)
    slot_pole = jnp.where(slot < live_counts[0], pole_order, -1)
    both = jnp.concatenate([leaf_lift[0], leaf_couple[0]], axis=0)
    in_both, out_poles, out_spread, diag = fold(
        slot_pole, leaf_diag, both, leaf_in, leaf_out, leaf_spread[0]
    )
    lifted, coupled = rise(in_both, poles, rank)
    parts = exchange(lifted.reshape(devices, owned, rank))
    inside = tree(parts, inner_lift, inner_couple, inner_spread)
    inside, coupled = lax.optimization_barrier((inside, coupled))
    above = exchange(inside).reshape(columns, rank)
    cross = lax.ppermute(coupled, "leaf", [(i, i ^ 1) for i in range(leaves)])
    near = near_field(diag, poles, out_poles, cross)
    updated = fall(near, out_spread, above)
    merged = exchange(updated.reshape(devices, block_rows, columns))
    return merged.reshape(width, columns)


def solution(mesh):
    placed = (
        P(BOTH, None),
        P(BOTH),
        P(BOTH, None),
        P(BOTH, None),
        P(BOTH, None),
        P(BOTH, None),
        P(BOTH, None, None),
        P(BOTH, None, None),
        P(BOTH, None, None),
        P(),
        P(),
        P(),
    )
    return jax.shard_map(
        local, mesh=mesh, in_specs=placed, out_specs=P(BOTH, None), check_vma=False
    )
```

time: 135 us -> 117 us (0.87)
  matrix products: 21.1 us -> 0 us
  blocking collectives: 35.7 us -> 49.7 us
  Pallas kernels: 9.97 us -> 21.6 us
  waiting for transfers between devices: 34.7 us -> 27 us
  starting transfers between devices: 21.9 us -> 16 us
  local copies, waits for them, and re-layouts: 7.82 us -> 2.04 us
  other arithmetic: 2.14 us -> 0.01 us
    dot_general x7 -> x0, matrix products: 21.1 us -> none  [dot(): return lax.dot_general(a, b, dims, preferred_element_type=jnp.float32)]
    pallas_call x0 -> x4, Pallas kernels: none -> 14.6 us  [the longest x1 7.99 us: fold(): pl.pallas_call(fold_kernel, out_shape=(jax.ShapeDtypeStruct((2 * rank, wi...]
    all_to_all x1 -> x2, blocking collectives: 35.7 us -> 49.7 us  [exchange(): return lax.all_to_all(blocks, BOTH, split_axis=0, concat_axis=0, tiled=True)]
    all_to_all x3 -> x2, waiting for transfers between devices: 34.7 us -> 27 us  [exchange(): return lax.all_to_all(blocks, BOTH, split_axis=0, concat_axis=0, tiled=True)]
    unnamed x21 -> x19, local copies, waits for them, and re-layouts: 7.82 us -> 2.04 us
    all_to_all x3 -> x2, starting transfers between devices: 20.7 us -> 15.3 us  [exchange(): return lax.all_to_all(blocks, BOTH, split_axis=0, concat_axis=0, tiled=True)]
    pallas_call x1, Pallas kernels: 9.97 us -> 7.02 us  [tree(): pl.pallas_call(functools.partial(tree_kernel, levels), out_shape=jax.Shap...]
  transfers between devices with their start and end apart: 4 -> 3, of which waited for: 3 -> 2; matrix products, arithmetic and copies ran while one was open for 12% -> 0% of each run, Pallas kernels for 7% -> 11%
where the time goes in v2:
time: 117 us
  blocking collectives  49.7 us (42%)
  waiting for transfers between devices  27 us (23%)
  Pallas kernels  21.6 us (18%)
  starting transfers between devices  16 us (14%)
  local copies, waits for them, and re-layouts  2.04 us (2%)
    all_to_all x2, blocking collectives, exchange(): return lax.all_to_all(blocks, BOTH, split_axis=0, concat_axis=0, tiled=True)  49.7 us
    all_to_all x2, waiting for transfers between devices, exchange(): return lax.all_to_all(blocks, BOTH, split_axis=0, concat_axis=0, tiled=True)  27 us
    all_to_all x2, starting transfers between devices, exchange(): return lax.all_to_all(blocks, BOTH, split_axis=0, concat_axis=0, tiled=True)  15.3 us
    pallas_call x1, Pallas kernels, fold(): pl.pallas_call(fold_kernel, out_shape=(jax.ShapeDtypeStruct((2 * rank, wi...  7.99 us
    pallas_call x1, Pallas kernels, tree(): pl.pallas_call(functools.partial(tree_kernel, levels), out_shape=jax.Shap...  7.02 us
    pallas_call x1, Pallas kernels, near_field(): pl.pallas_call(near_kernel, out_shape=jax.ShapeDtypeStruct((width, column...  5.08 us
  transfers between devices with their start and end apart: 3, of which 2 were waited for; matrix products, arithmetic and copies ran while one was open for 0% of the time, Pallas kernels for 11%

profile of v2, /device:TPU:1, one launch (start us, length us, event | category | flops | bytes accessed | tf_op | source)
XLA Modules:
  0.0 117.2 jit_solution(2265254257763398459)
XLA Ops:
  0.0 0.0 copy-start.1
  0.0 0.0 copy-start.2
  0.0 0.0 copy-start.3
  0.0 11.5 %all-to-all-start = ((bf16[128,8,1024]{2,1,0:T(8,128)(2,1)}), bf16[128,8,1024]{2,1,0:T(8,128)(2,1)S(1)}, u32[]{:S(2)}, u32[]{:S(2)}) async-start(bf16[128,8,1024]{2,1,0:T(8,128)(2,1)} %bitcast.18), calls=%async_computation | async-start | bytes 4194304 | tf_op jit(solution)/shard_map/all_to_all | solution.py:17
  12.2 0.0 copy-done.6
  12.2 0.0 copy-done.7
  12.2 0.0 copy-done.8
  12.2 0.0 copy-done.1
  12.3 0.0 copy-done.2
  12.3 0.0 copy-done.3
  12.3 8.0 %fold.1 = (bf16[256,1024]{1,0:T(8,128)(2,1)S(1)}, bf16[1024,128]{1,0:T(8,128)(2,1)S(1)}, bf16[1024,128]{1,0:T(8,128)(2,1)S(1)}, bf16[1024,1024]{1,0:T(8,128)(2,1)}) custom-call(s32[1,1024]{1,0:T(1,128)S(1)} %compare_select_fusion.slot_ref, bf16[1024,1024]{1,0:T(8,128)(2,1)} %diag_hbm.1, bf16[256,128]{1,0:T(8,128)(2,1)S(1)} %pad_maximum_fusion.both_ref, ...), custom_call_target="tpu_custom_call" | custom-call | flops 5368709120 | bytes 6291456 | tf_op jit(solution)/shard_map/fold/pallas_call | solution.py:84
  20.3 0.7 copy-done.4
  21.0 21.0 %all-to-all-done = bf16[128,8,1024]{2,1,0:T(8,128)(2,1)S(1)} async-done(((bf16[128,8,1024]{2,1,0:T(8,128)(2,1)}), bf16[128,8,1024]{2,1,0:T(8,128)(2,1)S(1)}, u32[]{:S(2)}, u32[]{:S(2)}) %all-to-all-start) | async-done | bytes 2097184 | tf_op jit(solution)/shard_map/all_to_all | solution.py:17
  42.0 0.8 rise.1
  42.8 15.1 %all_to_all.20.parts_ref = bf16[128,8,128]{2,1,0:T(8,128)(2,1)S(1)} all-to-all(bf16[128,8,128]{2,1,0:T(8,128)(2,1)S(1)} %bitcast.15), channel_id=1, replica_groups=mesh['grp'=4,'leaf'=32] {'grp','leaf'}, dimensions={0} | all-to-all | bytes 524288 | tf_op jit(solution)/shard_map/all_to_all | solution.py:17
  57.9 7.0 %tree.1 = bf16[128,8,128]{2,1,0:T(8,128)(2,1)} custom-call(bf16[128,8,128]{2,1,0:T(8,128)(2,1)S(1)} %all_to_all.20.parts_ref, bf16[124,128,128]{2,1,0:T(8,128)(2,1)} %lift_hbm.1, bf16[126,128,128]{2,1,0:T(8,128)(2,1)} %couple_hbm.1, bf16[124,128,128]{2,1,0:T(8,128)(2,1)} %spread_hbm.1), custom_call_target="tpu_custom_call" | custom-call | flops 392167424 | bytes 13631488 | tf_op jit(solution)/shard_map/tree/pallas_call | solution.py:226
  64.9 0.7 collective-permute-start
  65.6 3.8 %all-to-all-start.2 = ((bf16[128,8,128]{2,1,0:T(8,128)(2,1)}), bf16[128,8,128]{2,1,0:T(8,128)(2,1)S(1)}, u32[]{:S(2)}, u32[]{:S(2)}) async-start(bf16[128,8,128]{2,1,0:T(8,128)(2,1)} %tree.1), calls=%async_computation.2 | async-start | bytes 524288 | tf_op jit(solution)/shard_map/all_to_all | solution.py:17
  69.4 0.0 collective-permute-done.cross_ref
  69.5 5.1 %near.1.near_ref = bf16[1024,1024]{1,0:T(8,128)(2,1)S(1)} custom-call(bf16[1024,1024]{1,0:T(8,128)(2,1)} %get-tuple-element.13.diag_hbm, bf16[1024,1024]{1,0:T(8,128)(2,1)} %bitcast.12, bf16[1024,128]{1,0:T(8,128)(2,1)S(1)} %copy-done.5, bf16[1024,128]{1,0:T(8,128)(2,1)S(1)} %collective-permute-done.cross_ref), custom_call_target="tpu_custom_call" | custom-call | flops 2415919104 | bytes 7340032 | tf_op jit(solution)/shard_map/near/pallas_call | solution.py:266
  74.5 6.0 %all-to-all-done.2 = bf16[128,8,128]{2,1,0:T(8,128)(2,1)S(1)} async-done(((bf16[128,8,128]{2,1,0:T(8,128)(2,1)}), bf16[128,8,128]{2,1,0:T(8,128)(2,1)S(1)}, u32[]{:S(2)}, u32[]{:S(2)}) %all-to-all-start.2) | async-done | bytes 262176 | tf_op jit(solution)/shard_map/all_to_all | solution.py:17
  80.5 0.7 fall.1
  81.2 34.7 %all_to_all.21 = bf16[128,8,1024]{2,1,0:T(8,128)(2,1)S(1)} all-to-all(bf16[128,8,1024]{2,1,0:T(8,128)(2,1)S(1)} %bitcast.13), channel_id=1, replica_groups=mesh['grp'=4,'leaf'=32] {'grp','leaf'}, dimensions={0} | all-to-all | bytes 4194304 | tf_op jit(solution)/shard_map/all_to_all | solution.py:17
  115.9 1.3 %copy.15 = bf16[1024,1024]{1,0:T(8,128)(2,1)} copy(bf16[1024,1024]{1,0:T(8,128)(2,1)S(1)} %bitcast.17) | data formatting | bytes 4194304
  (10 shorter events, 0.0 us)
Async XLA Ops:
  0.0 12.2 %copy-start.6 = (bf16[1,128,128]{2,1,0:T(8,128)(2,1)S(1)}, bf16[1,128,128]{2,1,0:T(8,128)(2,1)}, u32[]{:S(2)}) copy-start(bf16[1,128,128]{2,1,0:T(8,128)(2,1)} %param.19) | copy-start | bytes 98308
  0.0 12.2 %copy-start.7 = (bf16[1,128,128]{2,1,0:T(8,128)(2,1)S(1)}, bf16[1,128,128]{2,1,0:T(8,128)(2,1)}, u32[]{:S(2)}) copy-start(bf16[1,128,128]{2,1,0:T(8,128)(2,1)} %param.18) | copy-start | bytes 98308
  0.0 12.2 %copy-start.8 = (s32[1,1024]{1,0:T(1,128)S(1)}, s32[1,1024]{1,0:T(1,128)}, u32[]{:S(2)}) copy-start(s32[1,1024]{1,0:T(1,128)} %param.14) | copy-start | bytes 12292
  0.0 12.2 %copy-start.1 = (bf16[1024,128]{1,0:T(8,128)(2,1)S(1)}, bf16[1024,128]{1,0:T(8,128)(2,1)}, u32[]{:S(2)}) copy-start(bf16[1024,128]{1,0:T(8,128)(2,1)} %in_ref.1) | copy-start | bytes 786436
  0.0 12.2 %copy-start.2 = (bf16[1024,128]{1,0:T(8,128)(2,1)S(1)}, bf16[1024,128]{1,0:T(8,128)(2,1)}, u32[]{:S(2)}) copy-start(bf16[1024,128]{1,0:T(8,128)(2,1)} %out_ref.1) | copy-start | bytes 786436
  0.0 12.2 %copy-start.3 = (bf16[1,128,128]{2,1,0:T(8,128)(2,1)S(1)}, bf16[1,128,128]{2,1,0:T(8,128)(2,1)}, u32[]{:S(2)}) copy-start(bf16[1,128,128]{2,1,0:T(8,128)(2,1)} %param.20) | copy-start | bytes 98308
  0.0 42.0 %all-to-all-start = ((bf16[128,8,1024]{2,1,0:T(8,128)(2,1)}), bf16[128,8,1024]{2,1,0:T(8,128)(2,1)S(1)}, u32[]{:S(2)}, u32[]{:S(2)}) async-start(bf16[128,8,1024]{2,1,0:T(8,128)(2,1)} %bitcast.18), calls=%async_computation | async-start | bytes 4194304 | tf_op jit(solution)/shard_map/all_to_all | solution.py:17
  20.3 0.7 copy-start.4
  42.0 22.9 %copy-start = (bf16[128,8,1024]{2,1,0:T(8,128)(2,1)}, bf16[128,8,1024]{2,1,0:T(8,128)(2,1)S(1)}, u32[]{:S(2)}) copy-start(bf16[128,8,1024]{2,1,0:T(8,128)(2,1)S(1)} %all-to-all-done) | copy-start | bytes 6291460
  57.9 11.6 %copy-start.5 = (bf16[1024,128]{1,0:T(8,128)(2,1)S(1)}, bf16[1024,128]{1,0:T(8,128)(2,1)}, u32[]{:S(2)}) copy-start(bf16[1024,128]{1,0:T(8,128)(2,1)} %copy-done.4) | copy-start | bytes 786436
  64.9 4.5 %collective-permute-start = (bf16[1024,128]{1,0:T(8,128)(2,1)S(1)}, bf16[1024,128]{1,0:T(8,128)(2,1)S(1)}, u32[]{:S(2)}, u32[]{:S(2)}) collective-permute-start(bf16[1024,128]{1,0:T(8,128)(2,1)S(1)} %get-tuple-element.18), channel_id=1, source_target_pairs={{0,1},{1,0},{2,3},{3,2},{4,5},{5,4},{6,7},{7,6},{8,9},{9,8},{10,11... | collective-permute-start | bytes 786440 | tf_op jit(solution)/shard_map/ppermute | solution.py:337
  65.6 14.9 %all-to-all-start.2 = ((bf16[128,8,128]{2,1,0:T(8,128)(2,1)}), bf16[128,8,128]{2,1,0:T(8,128)(2,1)S(1)}, u32[]{:S(2)}, u32[]{:S(2)}) async-start(bf16[128,8,128]{2,1,0:T(8,128)(2,1)} %tree.1), calls=%async_computation.2 | async-start | bytes 524288 | tf_op jit(solution)/shard_map/all_to_all | solution.py:17

commit v3 on v2

--- a/solution.py
+++ b/solution.py
@@ -34,6 +34,7 @@
     return pl.CostEstimate(flops=flops, bytes_accessed=moved, transcendentals=0)
 
 
+COVER_FLOPS = 1 << 33
 FAR = pl.BlockSpec(memory_space=pltpu.HBM)
 INSIDE = pl.BlockSpec(memory_space=pltpu.VMEM)
 TILE = 256
@@ -41,12 +42,21 @@
 
 def fold_kernel(
     slot_ref, diag_hbm, both_ref, in_ref, out_ref, spread_ref,
-    in_both_ref, out_poles_ref, out_spread_ref, folded_hbm,
-    chosen, diag, folded, sems,
+    lift_hbm, couple_hbm, inner_spread_hbm,
+    in_both_ref, out_poles_ref, out_spread_ref, folded_hbm, up_hbm, down_hbm, top_ref,
+    chosen, diag, folded, lift, couple, spread, up, down, unit, sems,
 ):
     width = diag.shape[0]
     load = pltpu.make_async_copy(diag_hbm, diag, sems.at[0])
     load.start()
+    inner_loads = [
+        pltpu.make_async_copy(source, target, sems.at[1 + width // TILE + number])
+        for number, (source, target) in enumerate(
+            ((lift_hbm, lift), (couple_hbm, couple), (inner_spread_hbm, spread))
+        )
+    ]
+    for copy in inner_loads:
+        copy.start()
     slots = slot_ref[...]
     for low in range(0, width, TILE):
         pole = lax.broadcasted_iota(jnp.int32, (TILE, width), 0) + low
@@ -72,30 +82,91 @@
         )
         store.start()
         stores.append(store)
+    side = unit.shape[0]
+    row = lax.broadcasted_iota(jnp.int32, (side, side), 0)
+    column = lax.broadcasted_iota(jnp.int32, (side, side), 1)
+    unit[...] = jnp.where(row == column, 1.0, 0.0).astype(jnp.bfloat16)
+    for copy in inner_loads:
+        copy.wait()
+
+    top_ref[...] = couple[:2]
+
+    def square(first, second, third, fourth):
+        top = jnp.concatenate([first, second], axis=1)
+        return jnp.concatenate([top, jnp.concatenate([third, fourth], axis=1)], axis=0)
+
+    def transposed(matrix):
+        return dot(unit[...], matrix, NT).astype(jnp.bfloat16)
+
+    def quad(number, carry):
+        n = 4 * number
+        for low in (0, 2):
+            up[2 * number + low // 2] = transposed(
+                square(
+                    lift[n + low], lift[n + low + 1], couple[n + low + 2], couple[n + low + 3]
+                )
+            )
+        down[number] = transposed(square(spread[n], spread[n + 2], spread[n + 1], spread[n + 3]))
+        return carry
+
+    lax.fori_loop(0, down.shape[0], quad, 0)
+    for number, (source, target) in enumerate(((up, up_hbm), (down, down_hbm))):
+        store = pltpu.make_async_copy(source, target, sems.at[4 + width // TILE + number])
+        store.start()
+        stores.append(store)
     for store in stores:
         store.wait()
 
 
-def fold(slot_pole, leaf_diag, both, leaf_in, leaf_out, spread):
+def fold(
+    slot_pole, leaf_diag, both, leaf_in, leaf_out, spread, inner_lift, inner_couple, inner_spread
+):
     width = leaf_diag.shape[0]
     rank = leaf_in.shape[1]
+    nodes = inner_lift.shape[0]
+    up = (nodes // 2, 2 * rank, 2 * rank)
+    down = (nodes // 4, 2 * rank, 2 * rank)
     square = pltpu.VMEM((width, width), jnp.bfloat16)
     tall = jax.ShapeDtypeStruct((width, rank), jnp.bfloat16)
     return pl.pallas_call(
         fold_kernel,
         out_shape=(
             jax.ShapeDtypeStruct((2 * rank, width), jnp.bfloat16),
-            tall,
-            tall,
+            pltpu.HBM((width, rank), jnp.bfloat16),
+            pltpu.HBM((width, rank), jnp.bfloat16),
             pltpu.HBM((width, width), jnp.bfloat16),
+            pltpu.HBM(up, jnp.bfloat16),
+            pltpu.HBM(down, jnp.bfloat16),
+            jax.ShapeDtypeStruct((2, rank, rank), jnp.bfloat16),
         ),
-        in_specs=[INSIDE, FAR, INSIDE, INSIDE, INSIDE, INSIDE],
-        out_specs=(INSIDE, INSIDE, INSIDE, FAR),
-        scratch_shapes=[square, square, square, pltpu.SemaphoreType.DMA((1 + width // TILE,))],
-        compiler_params=kernel_options(32),
-        cost_estimate=cost(5 * width**3, 6 << 20),
+        in_specs=[INSIDE, FAR, INSIDE, INSIDE, INSIDE, INSIDE, FAR, FAR, FAR],
+        out_specs=(INSIDE, INSIDE, INSIDE, FAR, FAR, FAR, INSIDE),
+        scratch_shapes=[
+            square,
+            square,
+            square,
+            pltpu.VMEM(inner_lift.shape, jnp.bfloat16),
+            pltpu.VMEM(inner_couple.shape, jnp.bfloat16),
+            pltpu.VMEM(inner_spread.shape, jnp.bfloat16),
+            pltpu.VMEM(up, jnp.bfloat16),
+            pltpu.VMEM(down, jnp.bfloat16),
+            pltpu.VMEM((2 * rank, 2 * rank), jnp.bfloat16),
+            pltpu.SemaphoreType.DMA((6 + width // TILE,)),
+        ],
+        compiler_params=kernel_options(48),
+        cost_estimate=cost(8 * width**3, 30 << 20),
         name="fold",
-    )(slot_pole, in_hbm(leaf_diag), both, leaf_in, leaf_out, spread)
+    )(
+        slot_pole,
+        in_hbm(leaf_diag),
+        both,
+        leaf_in,
+        leaf_out,
+        spread,
+        in_hbm(inner_lift),
+        in_hbm(inner_couple),
+        in_hbm(inner_spread),
+    )
 
 
 def rise_kernel(rows_ref, poles_ref, lifted_ref, coupled_ref):
@@ -116,7 +187,7 @@
         in_specs=[INSIDE, INSIDE],
         out_specs=(INSIDE, INSIDE),
         compiler_params=kernel_options(16),
-        cost_estimate=cost(2 * rows.shape[0] * width * columns, 3 << 20),
+        cost_estimate=cost(COVER_FLOPS, 3 << 20),
         name="rise",
     )(rows, poles)
 
@@ -125,38 +196,10 @@
     return pltpu.with_memory_space_constraint(array, pltpu.HBM)
 
 
-def tree_kernel(
-    levels, parts_ref, lift_hbm, couple_hbm, spread_hbm, out_ref, lift, couple, spread, cross, sems
-):
+def tree_kernel(levels, parts_ref, up, down, top, out_ref, cross):
     inner = levels - 1
     count = 1 << inner
     rank = parts_ref.shape[2]
-    copies = {}
-    number = 0
-
-    def fetch(first, source, target, offset, start, stop):
-        nonlocal number
-        piece = pl.ds(start - offset, stop - start)
-        copy = pltpu.make_async_copy(source.at[piece], target.at[piece], sems.at[number])
-        copy.start()
-        copies.setdefault(first, []).append(copy)
-        number += 1
-
-    half, quarter, middle = count // 2, count // 4, count + count // 2
-    for first, start, stop in (
-        (count, count, middle),
-        (middle, middle, 2 * count),
-        (half, half, count),
-        (quarter, 2, half),
-    ):
-        fetch(("up", first), lift_hbm, lift, 4, max(start, 4), stop)
-        fetch(("up", first), couple_hbm, couple, 2, start, stop)
-    for start, stop in ((4, half), (half, count), (count, 2 * count)):
-        fetch(("down", start), spread_hbm, spread, 4, start, stop)
-
-    def arrived(way, node):
-        for copy in copies.get((way, node), ()):
-            copy.wait()
 
     def apart(first, second):
         first, second = split_rows(first), split_rows(second)
@@ -184,32 +227,21 @@
     for height in range(1, levels):
         nodes = 1 << (levels - height)
         for node in range(nodes, 2 * nodes, 2):
-            arrived("up", node)
             pair = apart(skeletons[node], skeletons[node + 1])
-            couples = beside(couple[node - 2], couple[node - 1])
             if height < inner:
-                lifts = beside(lift[node - 4], lift[node - 3])
-                both = dot(pair, jnp.concatenate([lifts, couples], axis=0), NT)
-                up, across = both[:, :rank], both[:, rank:]
-                skeletons[node // 2] = joined(up[: 2 * width] + up[2 * width :])
+                both = dot(pair, up[node // 2 - 2], NN)
+                lifted, across = both[:, :rank], both[:, rank:]
+                skeletons[node // 2] = joined(lifted[: 2 * width] + lifted[2 * width :])
             else:
-                across = dot(pair, couples, NT)
+                across = dot(pair, beside(top[0], top[1]), NT)
             cross[node - 1] = joined(across[: 2 * width])
             cross[node - 2] = joined(across[2 * width :])
     incoming = {2: cross[0], 3: cross[1]}
     for height in range(inner - 1, 0, -1):
         nodes = 1 << (levels - height)
         for node in range(nodes, 2 * nodes, 4):
-            arrived("down", node)
             pair = apart(incoming[node // 2], incoming[node // 2 + 1])
-            matrices = jnp.concatenate(
-                [
-                    beside(spread[node - 4], spread[node - 2]),
-                    beside(spread[node - 3], spread[node - 1]),
-                ],
-                axis=0,
-            )
-            both = dot(pair, matrices, NT)
+            both = dot(pair, down[node // 4 - 1], NN)
             for child in range(4):
                 rows = both[2 * width * (child // 2) :][: 2 * width]
                 value = joined(rows[:, rank * (child % 2) :][:, :rank])
@@ -220,25 +252,19 @@
         out_ref[2 * n + 1] = value
 
 
-def tree(parts, inner_lift, inner_couple, inner_spread):
+def tree(parts, up, down, top):
     devices, width, rank = parts.shape
     levels = devices.bit_length() - 1
     return pl.pallas_call(
         functools.partial(tree_kernel, levels),
         out_shape=jax.ShapeDtypeStruct(parts.shape, jnp.bfloat16),
-        in_specs=[INSIDE, FAR, FAR, FAR],
+        in_specs=[INSIDE] * 4,
         out_specs=INSIDE,
-        scratch_shapes=[
-            pltpu.VMEM(inner_lift.shape, jnp.bfloat16),
-            pltpu.VMEM(inner_couple.shape, jnp.bfloat16),
-            pltpu.VMEM(inner_spread.shape, jnp.bfloat16),
-            pltpu.VMEM((inner_couple.shape[0], width, rank), jnp.float32),
-            pltpu.SemaphoreType.DMA((11,)),
-        ],
-        compiler_params=kernel_options(20),
+        scratch_shapes=[pltpu.VMEM((devices - 2, width, rank), jnp.float32)],
+        compiler_params=kernel_options(4),
         cost_estimate=cost(4 * 374 * 16 * 128 * 128, 13 << 20),
         name="tree",
-    )(parts, in_hbm(inner_lift), in_hbm(inner_couple), in_hbm(inner_spread))
+    )(parts, up, down, top)
 
 
 def near_kernel(diag_hbm, poles_hbm, out_poles_ref, cross_ref, near_ref, diag, poles, sems):
@@ -326,12 +352,20 @@
     slot = lax.broadcasted_iota(jnp.int32, (1, width), 1)
     slot_pole = jnp.where(slot < live_counts[0], pole_order, -1)
     both = jnp.concatenate([leaf_lift[0], leaf_couple[0]], axis=0)
-    in_both, out_poles, out_spread, diag = fold(
-        slot_pole, leaf_diag, both, leaf_in, leaf_out, leaf_spread[0]
+    in_both, out_poles, out_spread, diag, up, down, top = fold(
+        slot_pole,
+        leaf_diag,
+        both,
+        leaf_in,
+        leaf_out,
+        leaf_spread[0],
+        inner_lift,
+        inner_couple,
+        inner_spread,
     )
     lifted, coupled = rise(in_both, poles, rank)
     parts = exchange(lifted.reshape(devices, owned, rank))
-    inside = tree(parts, inner_lift, inner_couple, inner_spread)
+    inside = tree(parts, up, down, top)
     inside, coupled = lax.optimization_barrier((inside, coupled))
     above = exchange(inside).reshape(columns, rank)
     cross = lax.ppermute(coupled, "leaf", [(i, i ^ 1) for i in range(leaves)])

time: 117 us -> 115 us (0.983)
  waiting for transfers between devices: 27 us -> 12.5 us
  Pallas kernels: 21.6 us -> 33.2 us
    pallas_call x1, Pallas kernels: 7.99 us -> 23.1 us  [fold(): pl.pallas_call(fold_kernel, out_shape=(jax.ShapeDtypeStruct((2 * rank, wi...]
    all_to_all x2, waiting for transfers between devices: 27 us -> 12.5 us  [exchange(): return lax.all_to_all(blocks, BOTH, split_axis=0, concat_axis=0, tiled=True)]
    pallas_call x1, Pallas kernels: 7.02 us -> 3.4 us  [tree(): pl.pallas_call(functools.partial(tree_kernel, levels), out_shape=jax.Shap...]
  transfers between devices with their start and end apart: 3 -> 3, of which waited for: 2 -> 2; matrix products, arithmetic and copies ran while one was open for 0% -> 0% of each run, Pallas kernels for 11% -> 25%
where the time goes in v3:
time: 115 us; the launch traced here: 114 us
  blocking collectives  50 us (43%)
  Pallas kernels  33.2 us (29%)
  starting transfers between devices  15.9 us (14%)
  waiting for transfers between devices  12.5 us (11%)
  local copies, waits for them, and re-layouts  1.89 us (2%)
    all_to_all x2, blocking collectives, exchange(): return lax.all_to_all(blocks, BOTH, split_axis=0, concat_axis=0, tiled=True)  50 us
    pallas_call x1, Pallas kernels, fold(): pl.pallas_call(fold_kernel, out_shape=(jax.ShapeDtypeStruct((2 * rank, wi...  23.1 us
    all_to_all x2, starting transfers between devices, exchange(): return lax.all_to_all(blocks, BOTH, split_axis=0, concat_axis=0, tiled=True)  15.3 us
    all_to_all x2, waiting for transfers between devices, exchange(): return lax.all_to_all(blocks, BOTH, split_axis=0, concat_axis=0, tiled=True)  12.5 us
    pallas_call x1, Pallas kernels, near_field(): pl.pallas_call(near_kernel, out_shape=jax.ShapeDtypeStruct((width, column...  5.12 us
    pallas_call x1, Pallas kernels, tree(): pl.pallas_call(functools.partial(tree_kernel, levels), out_shape=jax.Shap...  3.4 us
  transfers between devices with their start and end apart: 3, of which 2 were waited for; matrix products, arithmetic and copies ran while one was open for 0% of the time, Pallas kernels for 25%

profile of v3, /device:TPU:1, one launch (start us, length us, event | category | flops | bytes accessed | tf_op | source)
XLA Modules:
  0.0 114.3 jit_solution(627768156760671475)
XLA Ops:
  0.0 0.0 copy-start.3
  0.0 0.0 copy-start.4
  0.0 0.0 copy-start.5
  0.0 11.5 %all-to-all-start = ((bf16[128,8,1024]{2,1,0:T(8,128)(2,1)}), bf16[128,8,1024]{2,1,0:T(8,128)(2,1)S(1)}, u32[]{:S(2)}, u32[]{:S(2)}) async-start(bf16[128,8,1024]{2,1,0:T(8,128)(2,1)} %bitcast.20), calls=%async_computation | async-start | bytes 4194304 | tf_op jit(solution)/shard_map/all_to_all | solution.py:17
  12.2 0.0 copy-done.7
  12.2 0.0 copy-done.8
  12.2 0.0 copy-done.9
  12.3 23.1 %fold.1 = (bf16[256,1024]{1,0:T(8,128)(2,1)S(1)}, bf16[1024,128]{1,0:T(8,128)(2,1)}, bf16[1024,128]{1,0:T(8,128)(2,1)}, bf16[1024,1024]{1,0:T(8,128)(2,1)}, bf16...) custom-call(s32[1,1024]{1,0:T(1,128)S(1)} %compare_select_fusion.slot_ref, ...), custom_call_target="tpu_custom_call" | custom-call | flops 8589934592 | bytes 31457280 | tf_op jit(solution)/shard_map/fold/pallas_call | solution.py:131
  35.4 6.6 %all-to-all-done = bf16[128,8,1024]{2,1,0:T(8,128)(2,1)S(1)} async-done(((bf16[128,8,1024]{2,1,0:T(8,128)(2,1)}), bf16[128,8,1024]{2,1,0:T(8,128)(2,1)S(1)}, u32[]{:S(2)}, u32[]{:S(2)}) %all-to-all-start) | async-done | bytes 2097184 | tf_op jit(solution)/shard_map/all_to_all | solution.py:17
  42.0 0.8 rise.1
  42.8 0.5 copy-done.1
  43.4 15.3 %all_to_all.20.parts_ref = bf16[128,8,128]{2,1,0:T(8,128)(2,1)S(1)} all-to-all(bf16[128,8,128]{2,1,0:T(8,128)(2,1)S(1)} %bitcast.17), channel_id=1, replica_groups=mesh['grp'=4,'leaf'=32] {'grp','leaf'}, dimensions={0} | all-to-all | bytes 524288 | tf_op jit(solution)/shard_map/all_to_all | solution.py:17
  58.7 0.0 slice-done
  58.7 0.0 copy-done
  58.7 3.4 %tree.1 = bf16[128,8,128]{2,1,0:T(8,128)(2,1)} custom-call(bf16[128,8,128]{2,1,0:T(8,128)(2,1)S(1)} %all_to_all.20.parts_ref, bf16[62,256,256]{2,1,0:T(8,128)(2,1)S(1)} %bitcast.13, bf16[31,256,256]{2,1,0:T(8,128)(2,1)S(1)} %copy-done, bf16[2,128,128]{2,1,0:T(8,128)(2,1)S(1)} %get-tuple-element.22.top), custom_call_target="tpu_custom_call" | custom-call | flops 392167424 | bytes 13631488 | tf_op jit(solution)/shard_map/tree/pallas_call | solution.py:258
  62.1 0.6 collective-permute-start
  62.7 3.8 %all-to-all-start.2 = ((bf16[128,8,128]{2,1,0:T(8,128)(2,1)}), bf16[128,8,128]{2,1,0:T(8,128)(2,1)S(1)}, u32[]{:S(2)}, u32[]{:S(2)}) async-start(bf16[128,8,128]{2,1,0:T(8,128)(2,1)} %tree.1), calls=%async_computation.2 | async-start | bytes 524288 | tf_op jit(solution)/shard_map/all_to_all | solution.py:17
  66.5 0.0 collective-permute-done.cross_ref
  66.6 5.1 %near.1.near_ref = bf16[1024,1024]{1,0:T(8,128)(2,1)S(1)} custom-call(bf16[1024,1024]{1,0:T(8,128)(2,1)} %get-tuple-element.16.diag_hbm, bf16[1024,1024]{1,0:T(8,128)(2,1)} %bitcast.15, bf16[1024,128]{1,0:T(8,128)(2,1)S(1)} %copy-done.6, bf16[1024,128]{1,0:T(8,128)(2,1)S(1)} %collective-permute-done.cross_ref), custom_call_target="tpu_custom_call" | custom-call | flops 2415919104 | bytes 7340032 | tf_op jit(solution)/shard_map/near/pallas_call | solution.py:292
  71.7 5.9 %all-to-all-done.2 = bf16[128,8,128]{2,1,0:T(8,128)(2,1)S(1)} async-done(((bf16[128,8,128]{2,1,0:T(8,128)(2,1)}), bf16[128,8,128]{2,1,0:T(8,128)(2,1)S(1)}, u32[]{:S(2)}, u32[]{:S(2)}) %all-to-all-start.2) | async-done | bytes 262176 | tf_op jit(solution)/shard_map/all_to_all | solution.py:17
  77.6 0.0 copy-done.2
  77.6 0.7 fall.1
  78.3 34.7 %all_to_all.21 = bf16[128,8,1024]{2,1,0:T(8,128)(2,1)S(1)} all-to-all(bf16[128,8,1024]{2,1,0:T(8,128)(2,1)S(1)} %bitcast.11), channel_id=1, replica_groups=mesh['grp'=4,'leaf'=32] {'grp','leaf'}, dimensions={0} | all-to-all | bytes 4194304 | tf_op jit(solution)/shard_map/all_to_all | solution.py:17
  113.0 1.3 %copy.15 = bf16[1024,1024]{1,0:T(8,128)(2,1)} copy(bf16[1024,1024]{1,0:T(8,128)(2,1)S(1)} %bitcast.19) | data formatting | bytes 4194304
  (17 shorter events, 0.0 us)
Async XLA Ops:
  0.0 12.2 %copy-start.7 = (bf16[1,128,128]{2,1,0:T(8,128)(2,1)S(1)}, bf16[1,128,128]{2,1,0:T(8,128)(2,1)}, u32[]{:S(2)}) copy-start(bf16[1,128,128]{2,1,0:T(8,128)(2,1)} %param.19) | copy-start | bytes 98308
  0.0 12.2 %copy-start.8 = (bf16[1,128,128]{2,1,0:T(8,128)(2,1)S(1)}, bf16[1,128,128]{2,1,0:T(8,128)(2,1)}, u32[]{:S(2)}) copy-start(bf16[1,128,128]{2,1,0:T(8,128)(2,1)} %param.18) | copy-start | bytes 98308
  0.0 12.2 %copy-start.9 = (s32[1,1024]{1,0:T(1,128)S(1)}, s32[1,1024]{1,0:T(1,128)}, u32[]{:S(2)}) copy-start(s32[1,1024]{1,0:T(1,128)} %param.14) | copy-start | bytes 12292
  0.0 12.2 %copy-start.3 = (bf16[1024,128]{1,0:T(8,128)(2,1)S(1)}, bf16[1024,128]{1,0:T(8,128)(2,1)}, u32[]{:S(2)}) copy-start(bf16[1024,128]{1,0:T(8,128)(2,1)} %in_ref.1) | copy-start | bytes 786436
  0.0 12.2 %copy-start.4 = (bf16[1024,128]{1,0:T(8,128)(2,1)S(1)}, bf16[1024,128]{1,0:T(8,128)(2,1)}, u32[]{:S(2)}) copy-start(bf16[1024,128]{1,0:T(8,128)(2,1)} %out_ref.1) | copy-start | bytes 786436
  0.0 12.2 %copy-start.5 = (bf16[1,128,128]{2,1,0:T(8,128)(2,1)S(1)}, bf16[1,128,128]{2,1,0:T(8,128)(2,1)}, u32[]{:S(2)}) copy-start(bf16[1,128,128]{2,1,0:T(8,128)(2,1)} %param.20) | copy-start | bytes 98308
  0.0 42.0 %all-to-all-start = ((bf16[128,8,1024]{2,1,0:T(8,128)(2,1)}), bf16[128,8,1024]{2,1,0:T(8,128)(2,1)S(1)}, u32[]{:S(2)}, u32[]{:S(2)}) async-start(bf16[128,8,1024]{2,1,0:T(8,128)(2,1)} %bitcast.20), calls=%async_computation | async-start | bytes 4194304 | tf_op jit(solution)/shard_map/all_to_all | solution.py:17
  42.0 1.4 %copy-start.1 = (bf16[128,8,1024]{2,1,0:T(8,128)(2,1)}, bf16[128,8,1024]{2,1,0:T(8,128)(2,1)S(1)}, u32[]{:S(2)}) copy-start(bf16[128,8,1024]{2,1,0:T(8,128)(2,1)S(1)} %all-to-all-done) | copy-start | bytes 6291460
  42.0 16.7 %slice-start = ((s8[8126464]{0:T(1024)(128)(4,1)}), s8[4194304]{0:T(1024)(128)(4,1)S(1)}, s32[]{:S(2)}) async-start(s8[8126464]{0:T(1024)(128)(4,1)} %bitcast.12), calls=%async_computation.4 | async-start | bytes 8388608
  42.0 16.7 %slice-start.1 = ((s8[8126464]{0:T(1024)(128)(4,1)}), s8[3932160]{0:T(1024)(128)(4,1)S(1)}, s32[]{:S(2)}) async-start(s8[8126464]{0:T(1024)(128)(4,1)} %bitcast.12), calls=%async_computation.5 | async-start | bytes 7864320
  42.0 16.7 %copy-start = (bf16[31,256,256]{2,1,0:T(8,128)(2,1)S(1)}, bf16[31,256,256]{2,1,0:T(8,128)(2,1)}, u32[]{:S(2)}) copy-start(bf16[31,256,256]{2,1,0:T(8,128)(2,1)} %get-tuple-element.21.down) | copy-start | bytes 12189700
  58.7 7.9 %copy-start.6 = (bf16[1024,128]{1,0:T(8,128)(2,1)S(1)}, bf16[1024,128]{1,0:T(8,128)(2,1)}, u32[]{:S(2)}) copy-start(bf16[1024,128]{1,0:T(8,128)(2,1)} %get-tuple-element.17.out_poles_ref) | copy-start | bytes 786436
  62.1 4.4 %collective-permute-start = (bf16[1024,128]{1,0:T(8,128)(2,1)S(1)}, bf16[1024,128]{1,0:T(8,128)(2,1)S(1)}, u32[]{:S(2)}, u32[]{:S(2)}) collective-permute-start(bf16[1024,128]{1,0:T(8,128)(2,1)S(1)} %get-tuple-element.24), channel_id=1, source_target_pairs={{0,1},{1,0},{2,3},{3,2},{4,5},{5,4},{6,7},{7,6},{8,9},{9,8},{10,11... | collective-permute-start | bytes 786440 | tf_op jit(solution)/shard_map/ppermute | solution.py:371
  62.7 14.9 %all-to-all-start.2 = ((bf16[128,8,128]{2,1,0:T(8,128)(2,1)}), bf16[128,8,128]{2,1,0:T(8,128)(2,1)S(1)}, u32[]{:S(2)}, u32[]{:S(2)}) async-start(bf16[128,8,128]{2,1,0:T(8,128)(2,1)} %tree.1), calls=%async_computation.2 | async-start | bytes 524288 | tf_op jit(solution)/shard_map/all_to_all | solution.py:17
  66.5 11.0 %copy-start.2 = (bf16[1024,128]{1,0:T(8,128)(2,1)S(1)}, bf16[1024,128]{1,0:T(8,128)(2,1)}, u32[]{:S(2)}) copy-start(bf16[1024,128]{1,0:T(8,128)(2,1)} %get-tuple-element.25.out_spread_ref) | copy-start | bytes 786436

commit v4 on v3

--- a/solution.py
+++ b/solution.py
@@ -267,23 +267,15 @@
     )(parts, up, down, top)
 
 
-def near_kernel(diag_hbm, poles_hbm, out_poles_ref, cross_ref, near_ref, diag, poles, sems):
-    width = diag.shape[0]
-    whole = pltpu.make_async_copy(poles_hbm, poles, sems.at[width // TILE])
-    whole.start()
-    loads = []
-    for number, low in enumerate(range(0, width, TILE)):
+def near_kernel(diag_hbm, poles_ref, out_poles_ref, cross_ref, near_ref, diag, sem):
+    load = pltpu.make_async_copy(diag_hbm, diag, sem)
+    load.start()
+    load.wait()
+    for low in range(0, poles_ref.shape[1], TILE):
         piece = pl.ds(low, TILE)
-        load = pltpu.make_async_copy(diag_hbm.at[piece], diag.at[piece], sems.at[number])
-        load.start()
-        loads.append(load)
-    whole.wait()
-    for number, low in enumerate(range(0, width, TILE)):
-        piece = pl.ds(low, TILE)
-        loads[number].wait()
-        value = dot(diag[piece], poles[...], NN)
-        value += dot(out_poles_ref[piece], cross_ref[...], NT)
-        near_ref[piece] = value.astype(near_ref.dtype)
+        value = dot(diag[...], poles_ref[:, piece], NN)
+        value += dot(out_poles_ref[...], cross_ref[piece], NT)
+        near_ref[:, piece] = value.astype(near_ref.dtype)
 
 
 def near_field(diag, poles, out_poles, cross):
@@ -292,17 +284,14 @@
     return pl.pallas_call(
         near_kernel,
         out_shape=jax.ShapeDtypeStruct((width, columns), jnp.bfloat16),
-        in_specs=[FAR, FAR, INSIDE, INSIDE],
+        in_specs=[FAR, INSIDE, INSIDE, INSIDE],
         out_specs=INSIDE,
-        scratch_shapes=[
-            pltpu.VMEM(diag.shape, jnp.bfloat16),
-            pltpu.VMEM(poles.shape, jnp.bfloat16),
-            pltpu.SemaphoreType.DMA((1 + width // TILE,)),
-        ],
+        input_output_aliases={1: 0},
+        scratch_shapes=[pltpu.VMEM(diag.shape, jnp.bfloat16), pltpu.SemaphoreType.DMA],
         compiler_params=kernel_options(24),
         cost_estimate=cost(2 * width * (width + rank) * columns, 7 << 20),
         name="near",
-    )(in_hbm(diag), in_hbm(poles), out_poles, cross)
+    )(in_hbm(diag), poles, out_poles, cross)
 
 
 def fall_kernel(near_ref, out_spread_ref, above_ref, out_ref):

time: 115 us -> 114 us (level)
  transfers between devices with their start and end apart: 3 -> 3, of which waited for: 2 -> 2; matrix products, arithmetic and copies ran while one was open for 0% -> 0% of each run, Pallas kernels for 25% -> 24%
where the time goes in v4:
time: 114 us
  blocking collectives  50 us (44%)
  Pallas kernels  32.6 us (29%)
  starting transfers between devices  15.9 us (14%)
  waiting for transfers between devices  13.1 us (11%)
  local copies, waits for them, and re-layouts  1.36 us (1%)
    all_to_all x2, blocking collectives, exchange(): return lax.all_to_all(blocks, BOTH, split_axis=0, concat_axis=0, tiled=True)  50 us
    pallas_call x1, Pallas kernels, fold(): pl.pallas_call(fold_kernel, out_shape=(jax.ShapeDtypeStruct((2 * rank, wi...  23.1 us
    all_to_all x2, starting transfers between devices, exchange(): return lax.all_to_all(blocks, BOTH, split_axis=0, concat_axis=0, tiled=True)  15.3 us
    all_to_all x2, waiting for transfers between devices, exchange(): return lax.all_to_all(blocks, BOTH, split_axis=0, concat_axis=0, tiled=True)  13.1 us
    pallas_call x1, Pallas kernels, near_field(): pl.pallas_call(near_kernel, out_shape=jax.ShapeDtypeStruct((width, column...  4.52 us
    pallas_call x1, Pallas kernels, tree(): pl.pallas_call(functools.partial(tree_kernel, levels), out_shape=jax.Shap...  3.39 us
  transfers between devices with their start and end apart: 3, of which 2 were waited for; matrix products, arithmetic and copies ran while one was open for 0% of the time, Pallas kernels for 24%

profile of v4, /device:TPU:1, one launch (start us, length us, event | category | flops | bytes accessed | tf_op | source)
XLA Modules:
  0.0 113.8 jit_solution(4102757496140540551)
XLA Ops:
  0.0 0.0 copy-start.2
  0.0 0.0 copy-start.3
  0.0 0.0 copy-start.4
  0.0 11.5 %all-to-all-start = ((bf16[128,8,1024]{2,1,0:T(8,128)(2,1)}), bf16[128,8,1024]{2,1,0:T(8,128)(2,1)S(1)}, u32[]{:S(2)}, u32[]{:S(2)}) async-start(bf16[128,8,1024]{2,1,0:T(8,128)(2,1)} %bitcast.20), calls=%async_computation | async-start | bytes 4194304 | tf_op jit(solution)/shard_map/all_to_all | solution.py:17
  12.2 0.0 copy-done.6
  12.2 0.0 copy-done.7
  12.2 0.0 copy-done.8
  12.2 0.0 copy-done.2
  12.3 23.1 %fold.1 = (bf16[256,1024]{1,0:T(8,128)(2,1)S(1)}, bf16[1024,128]{1,0:T(8,128)(2,1)}, bf16[1024,128]{1,0:T(8,128)(2,1)}, bf16[1024,1024]{1,0:T(8,128)(2,1)}, bf16...) custom-call(s32[1,1024]{1,0:T(1,128)S(1)} %compare_select_fusion.slot_ref, ...), custom_call_target="tpu_custom_call" | custom-call | flops 8589934592 | bytes 31457280 | tf_op jit(solution)/shard_map/fold/pallas_call | solution.py:131
  35.4 6.6 %all-to-all-done = bf16[128,8,1024]{2,1,0:T(8,128)(2,1)S(1)} async-done(((bf16[128,8,1024]{2,1,0:T(8,128)(2,1)}), bf16[128,8,1024]{2,1,0:T(8,128)(2,1)S(1)}, u32[]{:S(2)}, u32[]{:S(2)}) %all-to-all-start) | async-done | bytes 2097184 | tf_op jit(solution)/shard_map/all_to_all | solution.py:17
  42.0 0.8 rise.1
  42.8 15.3 %all_to_all.20.parts_ref = bf16[128,8,128]{2,1,0:T(8,128)(2,1)S(1)} all-to-all(bf16[128,8,128]{2,1,0:T(8,128)(2,1)S(1)} %bitcast.17), channel_id=1, replica_groups=mesh['grp'=4,'leaf'=32] {'grp','leaf'}, dimensions={0} | all-to-all | bytes 524288 | tf_op jit(solution)/shard_map/all_to_all | solution.py:17
  58.1 0.0 slice-done
  58.1 0.0 copy-done
  58.2 3.4 %tree.1 = bf16[128,8,128]{2,1,0:T(8,128)(2,1)} custom-call(bf16[128,8,128]{2,1,0:T(8,128)(2,1)S(1)} %all_to_all.20.parts_ref, bf16[62,256,256]{2,1,0:T(8,128)(2,1)S(1)} %bitcast.15, bf16[31,256,256]{2,1,0:T(8,128)(2,1)S(1)} %copy-done, bf16[2,128,128]{2,1,0:T(8,128)(2,1)S(1)} %get-tuple-element.22.top), custom_call_target="tpu_custom_call" | custom-call | flops 392167424 | bytes 13631488 | tf_op jit(solution)/shard_map/tree/pallas_call | solution.py:258
  61.6 0.6 collective-permute-start
  62.1 3.8 %all-to-all-start.2 = ((bf16[128,8,128]{2,1,0:T(8,128)(2,1)}), bf16[128,8,128]{2,1,0:T(8,128)(2,1)S(1)}, u32[]{:S(2)}, u32[]{:S(2)}) async-start(bf16[128,8,128]{2,1,0:T(8,128)(2,1)} %tree.1), calls=%async_computation.2 | async-start | bytes 524288 | tf_op jit(solution)/shard_map/all_to_all | solution.py:17
  66.0 0.0 collective-permute-done.cross_ref
  66.0 4.5 %near.1.near_ref = bf16[1024,1024]{1,0:T(8,128)(2,1)S(1)} custom-call(bf16[1024,1024]{1,0:T(8,128)(2,1)} %get-tuple-element.16.diag_hbm, bf16[1024,1024]{1,0:T(8,128)(2,1)S(1)} %bitcast.12, bf16[1024,128]{1,0:T(8,128)(2,1)S(1)} %copy-done.5, bf16[1024,128]{1,0:T(8,128)(2,1)S(1)} %collective-permute-done.cross_ref), custom_call_target="tpu_custom_call", output_to_operand_aliasing={{}: (1, {})} | custom-call | flops 2415919104 | bytes 7340032 | tf_op jit(solution)/shard_map/near/pallas_call | solution.py:284
  70.6 6.5 %all-to-all-done.2 = bf16[128,8,128]{2,1,0:T(8,128)(2,1)S(1)} async-done(((bf16[128,8,128]{2,1,0:T(8,128)(2,1)}), bf16[128,8,128]{2,1,0:T(8,128)(2,1)S(1)}, u32[]{:S(2)}, u32[]{:S(2)}) %all-to-all-start.2) | async-done | bytes 262176 | tf_op jit(solution)/shard_map/all_to_all | solution.py:17
  77.1 0.0 copy-done.1
  77.1 0.7 fall.1
  77.8 34.7 %all_to_all.21 = bf16[128,8,1024]{2,1,0:T(8,128)(2,1)S(1)} all-to-all(bf16[128,8,1024]{2,1,0:T(8,128)(2,1)S(1)} %bitcast.13), channel_id=1, replica_groups=mesh['grp'=4,'leaf'=32] {'grp','leaf'}, dimensions={0} | all-to-all | bytes 4194304 | tf_op jit(solution)/shard_map/all_to_all | solution.py:17
  112.5 1.3 %copy.17 = bf16[1024,1024]{1,0:T(8,128)(2,1)} copy(bf16[1024,1024]{1,0:T(8,128)(2,1)S(1)} %bitcast.19) | data formatting | bytes 4194304
  (15 shorter events, 0.0 us)
Async XLA Ops:
  0.0 12.2 %copy-start.6 = (bf16[1,128,128]{2,1,0:T(8,128)(2,1)S(1)}, bf16[1,128,128]{2,1,0:T(8,128)(2,1)}, u32[]{:S(2)}) copy-start(bf16[1,128,128]{2,1,0:T(8,128)(2,1)} %param.19) | copy-start | bytes 98308
  0.0 12.2 %copy-start.7 = (bf16[1,128,128]{2,1,0:T(8,128)(2,1)S(1)}, bf16[1,128,128]{2,1,0:T(8,128)(2,1)}, u32[]{:S(2)}) copy-start(bf16[1,128,128]{2,1,0:T(8,128)(2,1)} %param.18) | copy-start | bytes 98308
  0.0 12.2 %copy-start.8 = (s32[1,1024]{1,0:T(1,128)S(1)}, s32[1,1024]{1,0:T(1,128)}, u32[]{:S(2)}) copy-start(s32[1,1024]{1,0:T(1,128)} %param.14) | copy-start | bytes 12292
  0.0 12.2 %copy-start.2 = (bf16[1024,128]{1,0:T(8,128)(2,1)S(1)}, bf16[1024,128]{1,0:T(8,128)(2,1)}, u32[]{:S(2)}) copy-start(bf16[1024,128]{1,0:T(8,128)(2,1)} %in_ref.1) | copy-start | bytes 786436
  0.0 12.2 %copy-start.3 = (bf16[1024,128]{1,0:T(8,128)(2,1)S(1)}, bf16[1024,128]{1,0:T(8,128)(2,1)}, u32[]{:S(2)}) copy-start(bf16[1024,128]{1,0:T(8,128)(2,1)} %out_ref.1) | copy-start | bytes 786436
  0.0 12.2 %copy-start.4 = (bf16[1,128,128]{2,1,0:T(8,128)(2,1)S(1)}, bf16[1,128,128]{2,1,0:T(8,128)(2,1)}, u32[]{:S(2)}) copy-start(bf16[1,128,128]{2,1,0:T(8,128)(2,1)} %param.20) | copy-start | bytes 98308
  0.0 42.0 %all-to-all-start = ((bf16[128,8,1024]{2,1,0:T(8,128)(2,1)}), bf16[128,8,1024]{2,1,0:T(8,128)(2,1)S(1)}, u32[]{:S(2)}, u32[]{:S(2)}) async-start(bf16[128,8,1024]{2,1,0:T(8,128)(2,1)} %bitcast.20), calls=%async_computation | async-start | bytes 4194304 | tf_op jit(solution)/shard_map/all_to_all | solution.py:17
  42.0 16.1 %slice-start = ((s8[8126464]{0:T(1024)(128)(4,1)}), s8[4194304]{0:T(1024)(128)(4,1)S(1)}, s32[]{:S(2)}) async-start(s8[8126464]{0:T(1024)(128)(4,1)} %bitcast.14), calls=%async_computation.4 | async-start | bytes 8388608
  42.0 16.1 %slice-start.1 = ((s8[8126464]{0:T(1024)(128)(4,1)}), s8[3932160]{0:T(1024)(128)(4,1)S(1)}, s32[]{:S(2)}) async-start(s8[8126464]{0:T(1024)(128)(4,1)} %bitcast.14), calls=%async_computation.5 | async-start | bytes 7864320
  42.0 16.1 %copy-start = (bf16[31,256,256]{2,1,0:T(8,128)(2,1)S(1)}, bf16[31,256,256]{2,1,0:T(8,128)(2,1)}, u32[]{:S(2)}) copy-start(bf16[31,256,256]{2,1,0:T(8,128)(2,1)} %get-tuple-element.21.down) | copy-start | bytes 12189700
  58.2 7.9 %copy-start.5 = (bf16[1024,128]{1,0:T(8,128)(2,1)S(1)}, bf16[1024,128]{1,0:T(8,128)(2,1)}, u32[]{:S(2)}) copy-start(bf16[1024,128]{1,0:T(8,128)(2,1)} %get-tuple-element.17.out_poles_ref) | copy-start | bytes 786436
  61.6 4.4 %collective-permute-start = (bf16[1024,128]{1,0:T(8,128)(2,1)S(1)}, bf16[1024,128]{1,0:T(8,128)(2,1)S(1)}, u32[]{:S(2)}, u32[]{:S(2)}) collective-permute-start(bf16[1024,128]{1,0:T(8,128)(2,1)S(1)} %get-tuple-element.24), channel_id=1, source_target_pairs={{0,1},{1,0},{2,3},{3,2},{4,5},{5,4},{6,7},{7,6},{8,9},{9,8},{10,11... | collective-permute-start | bytes 786440 | tf_op jit(solution)/shard_map/ppermute | solution.py:360
  62.1 14.9 %all-to-all-start.2 = ((bf16[128,8,128]{2,1,0:T(8,128)(2,1)}), bf16[128,8,128]{2,1,0:T(8,128)(2,1)S(1)}, u32[]{:S(2)}, u32[]{:S(2)}) async-start(bf16[128,8,128]{2,1,0:T(8,128)(2,1)} %tree.1), calls=%async_computation.2 | async-start | bytes 524288 | tf_op jit(solution)/shard_map/all_to_all | solution.py:17
  66.0 11.0 %copy-start.1 = (bf16[1024,128]{1,0:T(8,128)(2,1)S(1)}, bf16[1024,128]{1,0:T(8,128)(2,1)}, u32[]{:S(2)}) copy-start(bf16[1024,128]{1,0:T(8,128)(2,1)} %get-tuple-element.25.out_spread_ref) | copy-start | bytes 786436

commit v5 on v4

--- a/solution.py
+++ b/solution.py
@@ -98,7 +98,7 @@
     def transposed(matrix):
         return dot(unit[...], matrix, NT).astype(jnp.bfloat16)
 
-    def quad(number, carry):
+    def quad(number):
         n = 4 * number
         for low in (0, 2):
             up[2 * number + low // 2] = transposed(
@@ -107,9 +107,16 @@
                 )
             )
         down[number] = transposed(square(spread[n], spread[n + 2], spread[n + 1], spread[n + 3]))
+
+    def several(step, carry):
+        for number in range(4):
+            quad(4 * step + number)
         return carry
 
-    lax.fori_loop(0, down.shape[0], quad, 0)
+    quads = down.shape[0]
+    lax.fori_loop(0, quads // 4, several, 0)
+    for number in range(quads // 4 * 4, quads):
+        quad(number)
     for number, (source, target) in enumerate(((up, up_hbm), (down, down_hbm))):
         store = pltpu.make_async_copy(source, target, sems.at[4 + width // TILE + number])
         store.start()

time: 114 us -> 114 us (level)
  Pallas kernels: 32.6 us -> 27.9 us
  waiting for transfers between devices: 13.1 us -> 17.8 us
    all_to_all x2, waiting for transfers between devices: 13.1 us -> 17.7 us  [exchange(): return lax.all_to_all(blocks, BOTH, split_axis=0, concat_axis=0, tiled=True)]
    pallas_call x1, Pallas kernels: 23.1 us -> 18.5 us  [fold(): pl.pallas_call(fold_kernel, out_shape=(jax.ShapeDtypeStruct((2 * rank, wi...]
  transfers between devices with their start and end apart: 3 -> 3, of which waited for: 2 -> 2; matrix products, arithmetic and copies ran while one was open for 0% -> 0% of each run, Pallas kernels for 24% -> 20%
where the time goes in v5:
time: 114 us
  blocking collectives  50 us (44%)
  Pallas kernels  27.9 us (24%)
  waiting for transfers between devices  17.8 us (16%)
  starting transfers between devices  15.9 us (14%)
  local copies, waits for them, and re-layouts  1.36 us (1%)
    all_to_all x2, blocking collectives, exchange(): return lax.all_to_all(blocks, BOTH, split_axis=0, concat_axis=0, tiled=True)  50 us
    pallas_call x1, Pallas kernels, fold(): pl.pallas_call(fold_kernel, out_shape=(jax.ShapeDtypeStruct((2 * rank, wi...  18.5 us
    all_to_all x2, waiting for transfers between devices, exchange(): return lax.all_to_all(blocks, BOTH, split_axis=0, concat_axis=0, tiled=True)  17.7 us
    all_to_all x2, starting transfers between devices, exchange(): return lax.all_to_all(blocks, BOTH, split_axis=0, concat_axis=0, tiled=True)  15.3 us
    pallas_call x1, Pallas kernels, near_field(): pl.pallas_call(near_kernel, out_shape=jax.ShapeDtypeStruct((width, column...  4.52 us
    pallas_call x1, Pallas kernels, tree(): pl.pallas_call(functools.partial(tree_kernel, levels), out_shape=jax.Shap...  3.39 us
  transfers between devices with their start and end apart: 3, of which 2 were waited for; matrix products, arithmetic and copies ran while one was open for 0% of the time, Pallas kernels for 20%

profile of v5, /device:TPU:1, one launch (start us, length us, event | category | flops | bytes accessed | tf_op | source)
XLA Modules:
  0.0 113.8 jit_solution(10739297245103212184)
XLA Ops:
  0.0 0.0 copy-start.2
  0.0 0.0 copy-start.3
  0.0 0.0 copy-start.4
  0.0 11.5 %all-to-all-start = ((bf16[128,8,1024]{2,1,0:T(8,128)(2,1)}), bf16[128,8,1024]{2,1,0:T(8,128)(2,1)S(1)}, u32[]{:S(2)}, u32[]{:S(2)}) async-start(bf16[128,8,1024]{2,1,0:T(8,128)(2,1)} %bitcast.20), calls=%async_computation | async-start | bytes 4194304 | tf_op jit(solution)/shard_map/all_to_all | solution.py:17
  12.2 0.0 copy-done.6
  12.2 0.0 copy-done.7
  12.2 0.0 copy-done.8
  12.2 0.0 copy-done.2
  12.3 18.5 %fold.1 = (bf16[256,1024]{1,0:T(8,128)(2,1)S(1)}, bf16[1024,128]{1,0:T(8,128)(2,1)}, bf16[1024,128]{1,0:T(8,128)(2,1)}, bf16[1024,1024]{1,0:T(8,128)(2,1)}, bf16...) custom-call(s32[1,1024]{1,0:T(1,128)S(1)} %compare_select_fusion.slot_ref, ...), custom_call_target="tpu_custom_call" | custom-call | flops 8589934592 | bytes 31457280 | tf_op jit(solution)/shard_map/fold/pallas_call | solution.py:138
  30.8 11.2 %all-to-all-done = bf16[128,8,1024]{2,1,0:T(8,128)(2,1)S(1)} async-done(((bf16[128,8,1024]{2,1,0:T(8,128)(2,1)}), bf16[128,8,1024]{2,1,0:T(8,128)(2,1)S(1)}, u32[]{:S(2)}, u32[]{:S(2)}) %all-to-all-start) | async-done | bytes 2097184 | tf_op jit(solution)/shard_map/all_to_all | solution.py:17
  42.0 0.8 rise.1
  42.8 15.3 %all_to_all.20.parts_ref = bf16[128,8,128]{2,1,0:T(8,128)(2,1)S(1)} all-to-all(bf16[128,8,128]{2,1,0:T(8,128)(2,1)S(1)} %bitcast.17), channel_id=1, replica_groups=mesh['grp'=4,'leaf'=32] {'grp','leaf'}, dimensions={0} | all-to-all | bytes 524288 | tf_op jit(solution)/shard_map/all_to_all | solution.py:17
  58.1 0.0 slice-done
  58.1 0.0 copy-done
  58.2 3.4 %tree.1 = bf16[128,8,128]{2,1,0:T(8,128)(2,1)} custom-call(bf16[128,8,128]{2,1,0:T(8,128)(2,1)S(1)} %all_to_all.20.parts_ref, bf16[62,256,256]{2,1,0:T(8,128)(2,1)S(1)} %bitcast.15, bf16[31,256,256]{2,1,0:T(8,128)(2,1)S(1)} %copy-done, bf16[2,128,128]{2,1,0:T(8,128)(2,1)S(1)} %get-tuple-element.22.top), custom_call_target="tpu_custom_call" | custom-call | flops 392167424 | bytes 13631488 | tf_op jit(solution)/shard_map/tree/pallas_call | solution.py:265
  61.6 0.6 collective-permute-start
  62.1 3.8 %all-to-all-start.2 = ((bf16[128,8,128]{2,1,0:T(8,128)(2,1)}), bf16[128,8,128]{2,1,0:T(8,128)(2,1)S(1)}, u32[]{:S(2)}, u32[]{:S(2)}) async-start(bf16[128,8,128]{2,1,0:T(8,128)(2,1)} %tree.1), calls=%async_computation.2 | async-start | bytes 524288 | tf_op jit(solution)/shard_map/all_to_all | solution.py:17
  66.0 0.0 collective-permute-done.cross_ref
  66.0 4.5 %near.1.near_ref = bf16[1024,1024]{1,0:T(8,128)(2,1)S(1)} custom-call(bf16[1024,1024]{1,0:T(8,128)(2,1)} %get-tuple-element.16.diag_hbm, bf16[1024,1024]{1,0:T(8,128)(2,1)S(1)} %bitcast.12, bf16[1024,128]{1,0:T(8,128)(2,1)S(1)} %copy-done.5, bf16[1024,128]{1,0:T(8,128)(2,1)S(1)} %collective-permute-done.cross_ref), custom_call_target="tpu_custom_call", output_to_operand_aliasing={{}: (1, {})} | custom-call | flops 2415919104 | bytes 7340032 | tf_op jit(solution)/shard_map/near/pallas_call | solution.py:291
  70.6 6.5 %all-to-all-done.2 = bf16[128,8,128]{2,1,0:T(8,128)(2,1)S(1)} async-done(((bf16[128,8,128]{2,1,0:T(8,128)(2,1)}), bf16[128,8,128]{2,1,0:T(8,128)(2,1)S(1)}, u32[]{:S(2)}, u32[]{:S(2)}) %all-to-all-start.2) | async-done | bytes 262176 | tf_op jit(solution)/shard_map/all_to_all | solution.py:17
  77.1 0.0 copy-done.1
  77.1 0.7 fall.1
  77.8 34.7 %all_to_all.21 = bf16[128,8,1024]{2,1,0:T(8,128)(2,1)S(1)} all-to-all(bf16[128,8,1024]{2,1,0:T(8,128)(2,1)S(1)} %bitcast.13), channel_id=1, replica_groups=mesh['grp'=4,'leaf'=32] {'grp','leaf'}, dimensions={0} | all-to-all | bytes 4194304 | tf_op jit(solution)/shard_map/all_to_all | solution.py:17
  112.5 1.3 %copy.17 = bf16[1024,1024]{1,0:T(8,128)(2,1)} copy(bf16[1024,1024]{1,0:T(8,128)(2,1)S(1)} %bitcast.19) | data formatting | bytes 4194304
  (15 shorter events, 0.0 us)
Async XLA Ops:
  0.0 12.2 %copy-start.6 = (bf16[1,128,128]{2,1,0:T(8,128)(2,1)S(1)}, bf16[1,128,128]{2,1,0:T(8,128)(2,1)}, u32[]{:S(2)}) copy-start(bf16[1,128,128]{2,1,0:T(8,128)(2,1)} %param.19) | copy-start | bytes 98308
  0.0 12.2 %copy-start.7 = (bf16[1,128,128]{2,1,0:T(8,128)(2,1)S(1)}, bf16[1,128,128]{2,1,0:T(8,128)(2,1)}, u32[]{:S(2)}) copy-start(bf16[1,128,128]{2,1,0:T(8,128)(2,1)} %param.18) | copy-start | bytes 98308
  0.0 12.2 %copy-start.8 = (s32[1,1024]{1,0:T(1,128)S(1)}, s32[1,1024]{1,0:T(1,128)}, u32[]{:S(2)}) copy-start(s32[1,1024]{1,0:T(1,128)} %param.14) | copy-start | bytes 12292
  0.0 12.2 %copy-start.2 = (bf16[1024,128]{1,0:T(8,128)(2,1)S(1)}, bf16[1024,128]{1,0:T(8,128)(2,1)}, u32[]{:S(2)}) copy-start(bf16[1024,128]{1,0:T(8,128)(2,1)} %in_ref.1) | copy-start | bytes 786436
  0.0 12.2 %copy-start.3 = (bf16[1024,128]{1,0:T(8,128)(2,1)S(1)}, bf16[1024,128]{1,0:T(8,128)(2,1)}, u32[]{:S(2)}) copy-start(bf16[1024,128]{1,0:T(8,128)(2,1)} %out_ref.1) | copy-start | bytes 786436
  0.0 12.2 %copy-start.4 = (bf16[1,128,128]{2,1,0:T(8,128)(2,1)S(1)}, bf16[1,128,128]{2,1,0:T(8,128)(2,1)}, u32[]{:S(2)}) copy-start(bf16[1,128,128]{2,1,0:T(8,128)(2,1)} %param.20) | copy-start | bytes 98308
  0.0 42.0 %all-to-all-start = ((bf16[128,8,1024]{2,1,0:T(8,128)(2,1)}), bf16[128,8,1024]{2,1,0:T(8,128)(2,1)S(1)}, u32[]{:S(2)}, u32[]{:S(2)}) async-start(bf16[128,8,1024]{2,1,0:T(8,128)(2,1)} %bitcast.20), calls=%async_computation | async-start | bytes 4194304 | tf_op jit(solution)/shard_map/all_to_all | solution.py:17
  42.0 16.1 %slice-start = ((s8[8126464]{0:T(1024)(128)(4,1)}), s8[4194304]{0:T(1024)(128)(4,1)S(1)}, s32[]{:S(2)}) async-start(s8[8126464]{0:T(1024)(128)(4,1)} %bitcast.14), calls=%async_computation.4 | async-start | bytes 8388608
  42.0 16.1 %slice-start.1 = ((s8[8126464]{0:T(1024)(128)(4,1)}), s8[3932160]{0:T(1024)(128)(4,1)S(1)}, s32[]{:S(2)}) async-start(s8[8126464]{0:T(1024)(128)(4,1)} %bitcast.14), calls=%async_computation.5 | async-start | bytes 7864320
  42.0 16.1 %copy-start = (bf16[31,256,256]{2,1,0:T(8,128)(2,1)S(1)}, bf16[31,256,256]{2,1,0:T(8,128)(2,1)}, u32[]{:S(2)}) copy-start(bf16[31,256,256]{2,1,0:T(8,128)(2,1)} %get-tuple-element.21.down) | copy-start | bytes 12189700
  58.2 7.9 %copy-start.5 = (bf16[1024,128]{1,0:T(8,128)(2,1)S(1)}, bf16[1024,128]{1,0:T(8,128)(2,1)}, u32[]{:S(2)}) copy-start(bf16[1024,128]{1,0:T(8,128)(2,1)} %get-tuple-element.17.out_poles_ref) | copy-start | bytes 786436
  61.6 4.4 %collective-permute-start = (bf16[1024,128]{1,0:T(8,128)(2,1)S(1)}, bf16[1024,128]{1,0:T(8,128)(2,1)S(1)}, u32[]{:S(2)}, u32[]{:S(2)}) collective-permute-start(bf16[1024,128]{1,0:T(8,128)(2,1)S(1)} %get-tuple-element.24), channel_id=1, source_target_pairs={{0,1},{1,0},{2,3},{3,2},{4,5},{5,4},{6,7},{7,6},{8,9},{9,8},{10,11... | collective-permute-start | bytes 786440 | tf_op jit(solution)/shard_map/ppermute | solution.py:367
  62.1 14.9 %all-to-all-start.2 = ((bf16[128,8,128]{2,1,0:T(8,128)(2,1)}), bf16[128,8,128]{2,1,0:T(8,128)(2,1)S(1)}, u32[]{:S(2)}, u32[]{:S(2)}) async-start(bf16[128,8,128]{2,1,0:T(8,128)(2,1)} %tree.1), calls=%async_computation.2 | async-start | bytes 524288 | tf_op jit(solution)/shard_map/all_to_all | solution.py:17
  66.0 11.0 %copy-start.1 = (bf16[1024,128]{1,0:T(8,128)(2,1)S(1)}, bf16[1024,128]{1,0:T(8,128)(2,1)}, u32[]{:S(2)}) copy-start(bf16[1024,128]{1,0:T(8,128)(2,1)} %get-tuple-element.25.out_spread_ref) | copy-start | bytes 786436
